TPU v7x, 32 devices: a whole 2x2x4 slice. The times are simulated.
32 devices in a mesh: rep: 1, dp: 32 (over x, y, z, core).
Axes of the slice: x: 2, y: 2, z: 4, core: 2. Of those that a mesh axis runs over, the one named last changes fastest.
Arguments:
- x: bfloat16 [32, 2048, 1024], P(('rep', 'dp'))
- dy: bfloat16 [32, 2048, 1024], P(('rep', 'dp'))
- w_gate: bfloat16 [2, 1024, 5120], replicated
- w_up: bfloat16 [2, 1024, 5120], replicated
- w_down: bfloat16 [2, 5120, 1024], replicated
- m_w_gate: float32 [2, 1024, 5120], replicated
- m_w_up: float32 [2, 1024, 5120], replicated
- m_w_down: float32 [2, 5120, 1024], replicated
- v_w_gate: float32 [2, 1024, 5120], replicated
- v_w_up: float32 [2, 1024, 5120], replicated
- v_w_down: float32 [2, 5120, 1024], replicated
Outputs:
- output 1: bfloat16 [2, 1024, 5120], P('rep')
- output 2: bfloat16 [2, 1024, 5120], P('rep')
- output 3: bfloat16 [2, 5120, 1024], P('rep')
- output 4: float32 [2, 1024, 5120], P('rep')
- output 5: float32 [2, 1024, 5120], P('rep')
- output 6: float32 [2, 5120, 1024], P('rep')
- output 7: float32 [2, 1024, 5120], P('rep')
- output 8: float32 [2, 1024, 5120], P('rep')
- output 9: float32 [2, 5120, 1024], P('rep')
All inputs are finite; a program needn't handle non-finite values.
Results may differ from a plain program's by a relative error of at most 0.022.
Values are sent between devices in bfloat16 or wider.
A program may use at most 3 GiB of HBM per device.

v0:
```python
import jax
import jax.numpy as jnp
from jax import lax
from jax.sharding import PartitionSpec as P

NAMES = ("w_gate", "w_up", "w_down")


def matmul(a, w):
    return jnp.dot(a, w, preferred_element_type=jnp.float32).astype(jnp.bfloat16)


def normed(h):
    wide = h.astype(jnp.float32)
    scale = lax.rsqrt(jnp.mean(wide**2, -1, keepdims=True) + 1e-6)
    return (wide * scale).astype(jnp.bfloat16)


def layer(h, w):
    a = normed(h)
    gate = jnp.dot(a, w["w_gate"], preferred_element_type=jnp.float32)
    up = jnp.dot(a, w["w_up"], preferred_element_type=jnp.float32)
    return h + matmul((jax.nn.silu(gate) * up).astype(jnp.bfloat16), w["w_down"])


def adamw(w, m, v, g):
    m = 0.9 * m + 0.1 * g
    v = 0.95 * v + 0.05 * g * g
    step = m * lax.rsqrt(v + 1e-8) + 0.1 * w
    return (w - 0.02 * step).astype(jnp.bfloat16), m, v


def solution(mesh):
    def step(x, dy, *arrays):
        weights, m, v = (arrays[i : i + 3] for i in (0, 3, 6))
        layers = weights[0].shape[0]
        h, kept = x[0], []
        for number in range(layers):
            kept.append(h)
            h = layer(h, {name: w[number] for name, w in zip(NAMES, weights, strict=True)})
        by_h, summed = dy[0], [None] * layers
        for number in reversed(range(layers)):
            _, back = jax.vjp(lambda w, h: layer(h, w), {name: w[number] for name, w in zip(NAMES, weights, strict=True)}, kept[number])
            by_w, by_h = back(by_h)
            summed[number] = [lax.psum(by_w[name], "dp") for name in NAMES]
        gradients = [jnp.stack([summed[number][i] for number in range(layers)]).astype(jnp.float32) for i in range(3)]
        new = [adamw(w.astype(jnp.float32), m, v, g) for w, m, v, g in zip(weights, m, v, gradients, strict=True)]
        return tuple(one[which] for which in range(3) for one in new)

    return jax.shard_map(
        step,
        mesh=mesh,
        in_specs=(P(("rep", "dp"), None, None),) * 2 + (P(None, None, None),) * 9,
        out_specs=(P("rep", None, None),) * 9,
        check_vma=False,
    )
```

profile of v0, /device:TPU:0, one launch (start us, length us, event | category | flops | bytes accessed | tf_op | source)
XLA Modules:
  0.0 1656.9 jit_solution(10319853243995045647)
XLA Ops:
  7.2 0.0 all-reduce.3.cloned.1.call-start
  7.2 6.6 copy.20
  13.8 3.1 fusion.56
  16.9 0.0 copy-start.3
  16.9 6.5 copy.21
  23.4 29.8 %convolution_convert_fusion.1 = bf16[2048,5120]{1,0:T(8,128)(2,1)} fusion(bf16[2,5120,1024]{2,1,0:T(8,128)(2,1)} %param.15, bf16[1,2048,1024]{2,1,0:T(8,128)(2,1)} %param.12), kind=kOutput, calls=%fused_computation.55 | convolution fusion | flops 21485322240 | bytes 35651584 | tf_op jit(solution)/shard_map/transpose(jvp())/dot_general | solution.py:10
  53.1 30.0 %fusion.43 = f32[2048,5120]{1,0:T(8,128)} fusion(bf16[2,1024,5120]{2,1,0:T(8,128)(2,1)} %param.13, bf16[1,2048,1024]{2,1,0:T(8,128)(2,1)} %param.11, f32[2048]{0:T(1024)S(1)} %add_rsqrt_fusion), kind=kOutput, calls=%fused_computation.76 | convolution fusion | flops 21481127936 | bytes 56631296 | tf_op jit(solution)/shard_map/dot_general | solution.py:21
  83.2 0.0 copy-done.3
  83.2 49.5 %multiply_convert_fusion.1 = (bf16[2048,5120]{1,0:T(8,128)(2,1)}, f32[2048,5120]{1,0:T(8,128)}) fusion(f32[2048,5120]{1,0:T(8,128)} %fusion.43, bf16[2,1024,5120]{2,1,0:T(8,128)(2,1)} %param.14, bf16[1,2048,1024]{2,1,0:T(8,128)(2,1)} %param.11, f32[2048]{0:T(1024)S(1)} %add_rsqrt_fusion), kind=kOutput, calls=%fused_computation.44 | convolution fusion | flops 21544042496 | bytes 119545856 | tf_op jit(solution)/shard_map/dot_general | solution.py:22
  132.7 30.2 %fusion.60 = (f32[2048]{0:T(1024)S(1)}, bf16[2048,1024]{0,1:T(8,128)(2,1)}) fusion(bf16[2048,5120]{1,0:T(8,128)(2,1)} %get-tuple-element.24, bf16[2,5120,1024]{2,1,0:T(8,128)(2,1)} %param.15, bf16[1,2048,1024]{1,2,0:T(8,128)(2,1)} %copy.20), kind=kOutput, calls=%fused_computation.97 | convolution fusion | flops 21485320192 | bytes 39854080 | tf_op jit(solution)/shard_map/dot_general | solution.py:10
  162.8 0.0 copy-start.1
  162.8 29.9 %fusion.30 = f32[2048,5120]{1,0:T(8,128)} fusion(bf16[2,1024,5120]{2,1,0:T(8,128)(2,1)} %param.14, bf16[2048,1024]{0,1:T(8,128)(2,1)} %get-tuple-element.27, f32[2048]{0:T(1024)S(1)} %fusion.80), kind=kOutput, calls=%fused_computation.63 | convolution fusion | flops 21481127936 | bytes 56631296 | tf_op jit(solution)/shard_map/jvp()/dot_general | solution.py:22
  192.7 0.0 copy-done.1
  192.7 57.6 %fusion.14 = (bf16[2048,5120]{1,0:T(8,128)(2,1)}, f32[2048,5120]{1,0:T(8,128)}) fusion(f32[2048,5120]{1,0:T(8,128)} %fusion.30, bf16[2048,5120]{1,0:T(8,128)(2,1)} %convolution_convert_fusion.1, bf16[2,1024,5120]{2,1,0:T(8,128)(2,1)} %param.13, bf16[2048,1024]{0,1:T(8,128)(2,1)} %get-tuple-element.27, f32[2048]{0:T(1024)S(1)} %fusion.80), kind=kOutput, calls=%fused_computation.32 | convolution fusion | flops 21606957056 | bytes 140517376 | tf_op jit(solution)/shard_map/jvp()/dot_general | solution.py:21
  250.3 32.5 %fusion.27 = bf16[2048,1024]{0,1:T(8,128)(2,1)} fusion(bf16[2048,5120]{1,0:T(8,128)(2,1)} %convolution_convert_fusion.1, bf16[2,1024,5120]{2,1,0:T(8,128)(2,1)} %param.14, f32[2048,5120]{1,0:T(8,128)} %get-tuple-element.29), kind=kOutput, calls=%fused_computation.48 | convolution fusion | flops 21537751040 | bytes 77594624 | tf_op jit(solution)/shard_map/transpose(jvp())/dot_general | solution.py:22
  282.8 32.7 %convert_bitcast_fusion.2 = bf16[1,1024,5120]{2,1,0:T(8,128)(2,1)} fusion(bf16[2048,5120]{1,0:T(8,128)(2,1)} %convolution_convert_fusion.1, bf16[2048,1024]{0,1:T(8,128)(2,1)} %get-tuple-element.27, f32[2048]{0:T(1024)S(1)} %fusion.80, f32[2048,5120]{1,0:T(8,128)} %get-tuple-element.29), kind=kOutput, calls=%fused_computation.80 | convolution fusion | flops 21549285376 | bytes 77602816 | tf_op jit(solution)/shard_map/transpose(jvp())/dot_general | solution.py:22
  315.5 37.0 %convert_bitcast_fusion = bf16[1,5120,1024]{2,1,0:T(8,128)(2,1)} fusion(f32[2048,5120]{1,0:T(8,128)} %fusion.30, bf16[1,2048,1024]{2,1,0:T(8,128)(2,1)} %param.12, f32[2048,5120]{1,0:T(8,128)} %get-tuple-element.29), kind=kOutput, calls=%fused_computation.78 | convolution fusion | flops 21542993920 | bytes 98566144 | tf_op jit(solution)/shard_map/transpose(jvp())/dot_general | solution.py:10
  352.4 28.0 %convert_bitcast_fusion.4 = bf16[1,1024,5120]{2,1,0:T(8,128)(2,1)} fusion(bf16[2048,5120]{1,0:T(8,128)(2,1)} %get-tuple-element.28, bf16[2048,1024]{0,1:T(8,128)(2,1)} %get-tuple-element.27, f32[2048]{0:T(1024)S(1)} %fusion.80), kind=kOutput, calls=%fused_computation.82 | convolution fusion | flops 21481127936 | bytes 35659776 | tf_op jit(solution)/shard_map/transpose(jvp())/dot_general | solution.py:21
  380.5 0.0 copy-start.2
  380.5 0.0 copy-start
  380.5 30.6 %fusion.62 = (f32[2048]{0:T(1024)S(1)}, bf16[2048,1024]{0,1:T(8,128)(2,1)}) fusion(bf16[2048,1024]{0,1:T(8,128)(2,1)} %get-tuple-element.27, bf16[2048,1024]{0,1:T(8,128)(2,1)} %fusion.27, bf16[2048,5120]{1,0:T(8,128)(2,1)} %get-tuple-element.28, bf16[2,1024,5120]{2,1,0:T(8,128)(2,1)} %param.13), kind=kOutput, calls=%fused_computation.99 | convolution fusion | flops 21485320192 | bytes 44048384 | tf_op jit(solution)/shard_map/transpose(jvp())/dot_general | solution.py:21
  411.1 0.0 copy-done.2
  411.1 0.0 copy-done
  411.1 6.6 fusion.65
  417.8 29.5 %convolution_convert_fusion = bf16[2048,5120]{1,0:T(8,128)(2,1)} fusion(bf16[2048,1024]{0,1:T(8,128)(2,1)} %fusion.65, bf16[2,5120,1024]{2,1,0:T(8,128)(2,1)} %param.15), kind=kOutput, calls=%fused_computation.54 | convolution fusion | flops 21485322240 | bytes 35651584 | tf_op jit(solution)/shard_map/transpose(jvp())/dot_general | solution.py:10
  447.3 0.0 copy-start.4
  447.3 28.0 %convert_bitcast_fusion.1 = bf16[1,5120,1024]{2,1,0:T(8,128)(2,1)} fusion(bf16[2048,5120]{1,0:T(8,128)(2,1)} %get-tuple-element.24, bf16[2048,1024]{0,1:T(8,128)(2,1)} %fusion.65), kind=kOutput, calls=%fused_computation.79 | convolution fusion | flops 21480079360 | bytes 35651584 | tf_op jit(solution)/shard_map/transpose(jvp())/dot_general | solution.py:10
  475.2 0.0 copy-done.4
  475.2 32.7 %convert_bitcast_fusion.3 = bf16[1,1024,5120]{2,1,0:T(8,128)(2,1)} fusion(bf16[2048,5120]{1,0:T(8,128)(2,1)} %convolution_convert_fusion, f32[2048,5120]{1,0:T(8,128)} %fusion.43, bf16[1,2048,1024]{1,2,0:T(8,128)(2,1)} %copy.20, f32[2048]{0:T(1024)S(1)} %copy-done.4), kind=kOutput, calls=%fused_computation.81 | convolution fusion | flops 21549285376 | bytes 77602816 | tf_op jit(solution)/shard_map/transpose(jvp())/dot_general | solution.py:22
  507.9 44.0 %convert_bitcast_fusion.5 = bf16[1,1024,5120]{2,1,0:T(8,128)(2,1)} fusion(f32[2048,5120]{1,0:T(8,128)} %fusion.43, f32[2048,5120]{1,0:T(8,128)} %get-tuple-element.25, bf16[2048,5120]{1,0:T(8,128)(2,1)} %convolution_convert_fusion, bf16[1,2048,1024]{1,2,0:T(8,128)(2,1)} %copy.20, f32[2048]{0:T(1024)S(1)} %copy-done.4), kind=kOutput, calls=%fused_computation.83 | convolution fusion | flops 21601714176 | bytes 119545856 | tf_op jit(solution)/shard_map/transpose(jvp())/dot_general | solution.py:21
  551.9 0.0 all-reduce.3.cloned.1.call-update
  551.9 881.0 %all-reduce.3.cloned.1.call-done = (bf16[1,1024,5120]{2,1,0:T(8,128)(2,1)}, bf16[1,1024,5120]{2,1,0:T(8,128)(2,1)}, bf16[1,1024,5120]{2,1,0:T(8,128)(2,1)}, bf16...) async-done(((bf16[1,1024,5120]{2,1,0:T(8,128)(2,1)}, bf16[1,1024,5120]{2,1,0:T(8,128)(2,1)}, ...) | async-done | bytes 62914576 | tf_op jit(solution)/shard_map/psum | solution.py:45
  1432.9 72.1 %fusion.11 = (bf16[2,5120,1024]{2,1,0:T(8,128)(2,1)}, f32[2,5120,1024]{2,1,0:T(8,128)}, f32[2,5120,1024]{2,1,0:T(8,128)}) fusion(bf16[2,5120,1024]{2,1,0:T(8,128)(2,1)} %param.15, bf16[1,5120,1024]{2,1,0:T(8,128)(2,1)} %get-tuple-element.13, bf16[1,5120,1024]{2,1,0:T(8,128)(2,1)} %get-tuple-element.14, f32[2,5120,1024]{2,1,0:T(8,128)} %param.21, ...), kind=kLoop, calls=%fused_computation.29 | loop fusion | flops 199229440 | bytes 230686720 | tf_op jit(solution)/shard_map/convert_element_type | solution.py:30
  1505.0 144.5 %fusion.2 = (bf16[2,1024,5120]{2,1,0:T(8,128)(2,1)}, f32[2,1024,5120]{2,1,0:T(8,128)}, f32[2,1024,5120]{2,1,0:T(8,128)}, bf16[2,1024,5120]{2,1,0:T(8,128)(2,1)},...) fusion(bf16[2,1024,5120]{2,1,0:T(8,128)(2,1)} %param.13, bf16[1,1024,5120]{2,1,0:T(8,128)(2,1)} %get-tuple-element.9, ...), kind=kLoop, calls=%fused_computation.20 | loop fusion | flops 398458880 | bytes 461373440 | tf_op jit(solution)/shard_map/convert_element_type | solution.py:30
  (3 shorter events, 0.0 us)
Async XLA Ops:
  7.2 1425.7 %all-reduce.3.cloned.1.call-start = ((), (), s32[]{:S(2)}) async-start(), calls=%async_computation | async-start | bytes 125829120 | tf_op jit(solution)/shard_map/psum | solution.py:45
  16.9 66.3 %copy-start.3 = (f32[2048]{0:T(1024)}, f32[2048]{0:T(1024)S(1)}, u32[]{:S(2)}) copy-start(f32[2048]{0:T(1024)S(1)} %add_rsqrt_fusion) | copy-start | bytes 24580
  162.8 29.9 %copy-start.1 = (f32[2048]{0:T(1024)}, f32[2048]{0:T(1024)S(1)}, u32[]{:S(2)}) copy-start(f32[2048]{0:T(1024)S(1)} %get-tuple-element.26) | copy-start | bytes 24580
  380.5 30.6 %copy-start.2 = (f32[2048]{0:T(1024)S(1)}, f32[2048]{0:T(1024)}, u32[]{:S(2)}) copy-start(f32[2048]{0:T(1024)} %copy-done.1) | copy-start | bytes 24580
  380.5 30.6 %copy-start = (bf16[1,2048,1024]{1,2,0:T(8,128)(2,1)S(1)}, bf16[1,2048,1024]{1,2,0:T(8,128)(2,1)}, u32[]{:S(2)}) copy-start(bf16[1,2048,1024]{1,2,0:T(8,128)(2,1)} %copy.21) | copy-start | bytes 12582916
  447.3 28.0 %copy-start.4 = (f32[2048]{0:T(1024)S(1)}, f32[2048]{0:T(1024)}, u32[]{:S(2)}) copy-start(f32[2048]{0:T(1024)} %copy-done.3) | copy-start | bytes 24580
Sparse Core Ops, SparseCore 0:
  552.1 880.7 all-reduce.2
where the time goes:
time: 1660 us
  waiting for transfers between devices  881 us (53%)
  matrix products  522 us (31%)
  other arithmetic  226 us (14%)
    psum x1, waiting for transfers between devices, step(): summed[number] = [lax.psum(by_w[name], 'dp') for name in NAMES]  881 us
    convert_element_type x2, other arithmetic, adamw(): return ((w - 0.02 * step).astype(jnp.bfloat16), m, v)  217 us
    dot_general x5, matrix products, layer(): gate = jnp.dot(a, w['w_gate'], preferred_element_type=jnp.float32)  190 us
    dot_general x5, matrix products, layer(): up = jnp.dot(a, w['w_up'], preferred_element_type=jnp.float32)  177 us
    dot_general x5, matrix products, matmul(): jnp.dot(a, w, preferred_element_type=jnp.float32).astype(jnp.bfloat16)  154 us
  transfers between devices with their start and end apart: 1, of which 1 were waited for; matrix products, arithmetic and copies ran while one was open for 0% of the time, Pallas kernels for 0%

commit v1 on v0

v1 whole, which is shorter than its diff:
```python
import functools

import jax
import jax.numpy as jnp
from jax import lax
from jax.experimental import pallas as pl
from jax.experimental.pallas import tpu as pltpu
from jax.sharding import PartitionSpec as P

MESH = pl.DeviceIdType.MESH
F32, BF16 = jnp.float32, jnp.bfloat16
MIB = 1024 * 1024

CORE, Z0, Z1, Y, X = 1, 2, 4, 8, 16
BITS = (CORE, Z0, Z1, Y, X)
ORDERS = ((CORE, X, Y, Z0, Z1), (CORE, Y, X, Z0, Z1), (CORE, Z0, X, Y, Z1))
STAGES = 5
GROUP = 1 << STAGES
CHUNK = 512
LAG = 2
SLOTS = 2 * LAG
R_SLOTS = 16


def pick(color, values):
    out = values[-1]
    for k in range(len(values) - 2, -1, -1):
        out = jnp.where(color == k, values[k], out)
    return out


def position(order, device):
    return sum(((device // m) % 2) << (STAGES - 1 - i) for i, m in enumerate(order))


def owners(order):
    found = [0] * GROUP
    for device in range(GROUP):
        found[position(order, device)] = device
    return found


def params(limit=60, **more):
    return pltpu.CompilerParams(dimension_semantics=("arbitrary",), vmem_limit_bytes=limit * MIB, **more)


def dot(a, b):
    return jnp.dot(a, b, preferred_element_type=F32)


def dot_nt(a, b):
    return lax.dot_general(a, b, (((1,), (1,)), ((), ())), preferred_element_type=F32)


def once(shape, index):
    return pl.BlockSpec(shape, index, pipeline_mode=pl.Buffered(1))


def norm_in(h):
    wide = h.astype(F32)
    return (wide * lax.rsqrt(jnp.mean(wide**2, -1, keepdims=True) + 1e-6)).astype(BF16)


def normed(h):
    wide = h.astype(F32)
    scale = lax.rsqrt(jnp.mean(wide**2, -1, keepdims=True) + 1e-6)
    return (wide * scale).astype(BF16)


def forward_kernel(parts, h_ref, wg_ref, wu_ref, gate_ref, up_ref, mid_ref, a_ref):
    t = h_ref.shape[0] // parts

    @pl.when(pl.program_id(0) == 0)
    def _():
        for i in range(parts):
            a_ref[i * t : (i + 1) * t] = norm_in(h_ref[i * t : (i + 1) * t])

    for i in range(parts):
        rows = slice(i * t, (i + 1) * t)
        gate = dot(a_ref[rows], wg_ref[0])
        up = dot(a_ref[rows], wu_ref[0])
        gate_ref[rows] = gate
        up_ref[rows] = up
        mid_ref[rows] = (jax.nn.silu(gate) * up).astype(BF16)


def forward(h, w_gate, w_up, layer):
    tokens, d = h.shape
    ff = w_gate.shape[2]
    weight = pl.BlockSpec((1, d, CHUNK), lambda j: (layer, 0, j))
    tile = pl.BlockSpec((tokens, CHUNK), lambda j: (0, j))
    return pl.pallas_call(
        functools.partial(forward_kernel, 4),
        grid=(ff // CHUNK,),
        in_specs=[once((tokens, d), lambda j: (0, 0)), weight, weight],
        out_specs=[tile, tile, tile],
        out_shape=[jax.ShapeDtypeStruct((tokens, ff), t) for t in (F32, F32, BF16)],
        scratch_shapes=[pltpu.VMEM((tokens, d), BF16)],
        compiler_params=params(),
        cost_estimate=pl.CostEstimate(flops=4 * tokens * d * ff, bytes_accessed=10 * tokens * ff, transcendentals=tokens * ff),
        name="forward",
    )(h, w_gate, w_up)


def down_kernel(mid_ref, w_ref, h_ref, out_ref):
    out_ref[...] = h_ref[...] + dot(mid_ref[...], w_ref[0]).astype(BF16)


def down(mid, w_down, h, layer):
    tokens, ff = mid.shape
    d = h.shape[1]
    rows = 256
    return pl.pallas_call(
        down_kernel,
        grid=(tokens // rows,),
        in_specs=[
            pl.BlockSpec((rows, ff), lambda i: (i, 0)),
            once((1, ff, d), lambda i: (layer, 0, 0)),
            pl.BlockSpec((rows, d), lambda i: (i, 0)),
        ],
        out_specs=pl.BlockSpec((rows, d), lambda i: (i, 0)),
        out_shape=jax.ShapeDtypeStruct((tokens, d), BF16),
        compiler_params=params(),
        cost_estimate=pl.CostEstimate(flops=2 * tokens * d * ff, bytes_accessed=2 * (tokens + d) * ff, transcendentals=0),
        name="down",
    )(mid, w_down, h)


def through(gate, up, by_mid):
    by_mid = by_mid.astype(BF16).astype(F32)
    s = jax.nn.sigmoid(gate)
    silu = gate * s
    return (silu * up).astype(BF16), (by_mid * up * (s * (1 + gate * (1 - s)))).astype(BF16), (by_mid * silu).astype(BF16)


def turned(j, out_ref, first_ref, second_ref):
    width = out_ref.shape[1]
    at = lax.rem(j, 4) * width

    @pl.when(j < 4)
    def _():
        out_ref[0] = first_ref[:, pl.ds(pl.multiple_of(at, width), width)].T

    @pl.when((j >= 4) & (j < 8))
    def _():
        out_ref[0] = second_ref[:, pl.ds(pl.multiple_of(at, width), width)].T


def last_kernel(parts, h_ref, dy_ref, wg_ref, wu_ref, wd_ref, b_ref, at_ref, a_ref):
    t = h_ref.shape[0] // parts
    j = pl.program_id(0)

    @pl.when(j == 0)
    def _():
        for i in range(parts):
            a_ref[i * t : (i + 1) * t] = norm_in(h_ref[i * t : (i + 1) * t])

    turned(j, at_ref, dy_ref, a_ref)
    for i in range(parts):
        rows = slice(i * t, (i + 1) * t)
        gate = dot(a_ref[rows], wg_ref[0])
        up = dot(a_ref[rows], wu_ref[0])
        by_mid = dot_nt(dy_ref[rows], wd_ref[0])
        b_ref[0, rows], b_ref[1, rows], b_ref[2, rows] = through(gate, up, by_mid)


def middle_kernel(parts, h_ref, dy_ref, gate_ref, up_ref, wd_ref, b_ref, at_ref, a_ref):
    t = h_ref.shape[0] // parts
    j = pl.program_id(0)

    @pl.when(j == 0)
    def _():
        for i in range(parts):
            a_ref[i * t : (i + 1) * t] = norm_in(h_ref[i * t : (i + 1) * t])

    turned(j, at_ref, dy_ref, a_ref)
    for i in range(parts):
        rows = slice(i * t, (i + 1) * t)
        by_mid = dot_nt(dy_ref[rows], wd_ref[0])
        b_ref[0, rows], b_ref[1, rows], b_ref[2, rows] = through(gate_ref[rows], up_ref[rows], by_mid)


def backward_mid(h, dy, layer, w_down, kept=None, weights=None):
    tokens, d = h.shape
    ff = w_down.shape[1]
    whole = once((tokens, d), lambda j: (0, 0))
    tile = pl.BlockSpec((tokens, CHUNK), lambda j: (0, j))
    weight = pl.BlockSpec((1, d, CHUNK), lambda j: (layer, 0, j))
    turn = lambda j: (jnp.minimum(j // 4, 1), jnp.where(j < 8, lax.rem(j, 4), 3), 0)
    return pl.pallas_call(
        functools.partial(last_kernel if kept is None else middle_kernel, 4),
        grid=(ff // CHUNK,),
        in_specs=[whole, whole]
        + ([weight, weight] if kept is None else [tile, tile])
        + [pl.BlockSpec((1, CHUNK, d), lambda j: (layer, j, 0))],
        out_specs=[pl.BlockSpec((3, tokens, CHUNK), lambda j: (0, 0, j)), pl.BlockSpec((1, d // 4, tokens), turn)],
        out_shape=[jax.ShapeDtypeStruct((3, tokens, ff), BF16), jax.ShapeDtypeStruct((2, d, tokens), BF16)],
        scratch_shapes=[pltpu.VMEM((tokens, d), BF16)],
        compiler_params=params(),
        cost_estimate=pl.CostEstimate(
            flops=(6 if kept is None else 2) * tokens * d * ff, bytes_accessed=14 * tokens * ff, transcendentals=tokens * ff
        ),
        name="last" if kept is None else "middle",
    )(h, dy, *(weights if kept is None else kept), w_down)


def gradient_kernel(n_c, per, with_da, *refs):
    at_ref, b_ref = refs[:2]
    refs = refs[2:]
    if with_da:
        wg_ref, wu_ref, out_ref, da_ref = refs[:4]
        refs = refs[4:]
    else:
        out_ref = refs[0]
        refs = refs[1:]
    s_refs, k_refs, r_refs = refs[:STAGES], refs[STAGES : 2 * STAGES], refs[2 * STAGES : 3 * STAGES]
    send_sem, recv_sem = refs[3 * STAGES : 3 * STAGES + 2]
    rows = out_ref.shape[1]
    j = pl.program_id(0)
    me = lax.axis_index("dp")
    bits = {m: lax.rem(lax.div(me, m), 2) for m in BITS}
    peers = {m: me + m * (1 - 2 * bits[m]) for m in BITS}

    @pl.when(j == 0)
    def _():
        barrier = pltpu.get_barrier_semaphore()
        for m in BITS:
            pl.semaphore_signal(barrier, inc=1, device_id={"dp": peers[m]}, device_id_type=MESH)
        pl.semaphore_wait(barrier, len(BITS))

    def copy(stage, c):
        slot = lax.rem(c, SLOTS)
        r_slot = lax.rem(c, R_SLOTS)
        return pltpu.make_async_remote_copy(
            src_ref=s_refs[stage].at[slot],
            dst_ref=r_refs[stage].at[r_slot],
            send_sem=send_sem.at[stage, slot],
            recv_sem=recv_sem.at[stage, r_slot],
            device_id={"dp": pick(lax.rem(c, len(ORDERS)), [peers[o[stage]] for o in ORDERS])},
            device_id_type=MESH,
        )

    for s in reversed(range(STAGES)):
        c = j - (s + 1) * LAG

        @pl.when((c >= 0) & (c < n_c))
        def _(s=s, c=c):
            k_slot = lax.rem(c, LAG + 1)
            r_slot = lax.rem(c, R_SLOTS)
            came = copy(s, c)
            came.wait_send()
            came.wait_recv()
            if s == STAGES - 1:
                out_ref[0] = (k_refs[s][k_slot] + r_refs[s][r_slot].astype(F32)).astype(BF16)
            else:
                half = 2 ** (STAGES - 2 - s) * rows
                bit = pick(lax.rem(c, len(ORDERS)), [bits[o[s + 1]] for o in ORDERS])
                give = pl.ds(pl.multiple_of((1 - bit) * half, half), half)
                keep = pl.ds(pl.multiple_of(bit * half, half), half)
                s_refs[s + 1][lax.rem(c, SLOTS)] = (k_refs[s][k_slot, give] + r_refs[s][r_slot, give].astype(F32)).astype(BF16)
                k_refs[s + 1][k_slot] = k_refs[s][k_slot, keep] + r_refs[s][r_slot, keep].astype(F32)
                copy(s + 1, c).start()

    @pl.when(j < n_c)
    def _():
        core = bits[CORE]
        s_refs[0][lax.rem(j, SLOTS)] = dot(at_ref[0, 1 - core], b_ref[0]).astype(BF16)
        copy(0, j).start()
        k_refs[0][lax.rem(j, LAG + 1)] = dot(at_ref[0, core], b_ref[0])

    if with_da:
        acc_ref, da_sem = refs[3 * STAGES + 2 :]
        parts = 4
        t = acc_ref.shape[0] // parts
        for first, w_ref, begin in ((True, wg_ref, per), (False, wu_ref, 2 * per)):

            @pl.when((j >= begin) & (j < begin + per))
            def _(first=first, w_ref=w_ref, begin=begin):
                for i in range(parts):
                    piece = slice(i * t, (i + 1) * t)
                    term = dot_nt(b_ref[0, piece], w_ref[0])
                    if first:

                        @pl.when(j == begin)
                        def _():
                            acc_ref[piece] = term

                        @pl.when(j > begin)
                        def _():
                            acc_ref[piece] += term

                    else:
                        acc_ref[piece] += term

        @pl.when(j == n_c)
        def _():
            pltpu.make_async_copy(acc_ref, da_ref, da_sem).start()

        @pl.when(j == n_c + STAGES * LAG - 1)
        def _():
            pltpu.make_async_copy(acc_ref, da_ref, da_sem).wait()


def gradients(at, b, collective_id, layer, weights=None):
    _, d, tokens = at.shape
    w, _, ff = b.shape
    per = ff // CHUNK
    n_c = w * per
    rows = d // GROUP
    sizes = [2 ** (STAGES - 1 - s) * rows for s in range(STAGES)]
    clip = lambda j: jnp.minimum(j, n_c - 1)
    done = lambda j: jnp.clip(j - STAGES * LAG, 0, n_c - 1)
    with_da = weights is not None
    in_specs = [
        pl.BlockSpec((1, 2, d // 2, tokens), lambda j: (jnp.where(j < per, 0, 1), 0, 0, 0)),
        pl.BlockSpec((1, tokens, CHUNK), lambda j: (clip(j) // per, 0, lax.rem(clip(j), per))),
    ]
    out_specs = [pl.BlockSpec((1, rows, CHUNK), lambda j: (done(j) // per, 0, lax.rem(done(j), per)))]
    out_shape = [jax.ShapeDtypeStruct((w, rows, ff), BF16)]
    scratch = (
        [pltpu.VMEM((SLOTS, n, CHUNK), BF16) for n in sizes]
        + [pltpu.VMEM((LAG + 1, n, CHUNK), F32) for n in sizes]
        + [pltpu.VMEM((R_SLOTS, n, CHUNK), BF16) for n in sizes]
        + [pltpu.SemaphoreType.DMA((STAGES, SLOTS)), pltpu.SemaphoreType.DMA((STAGES, R_SLOTS))]
    )
    if with_da:
        for begin in (per, 2 * per):
            in_specs.append(pl.BlockSpec((1, d, CHUNK), lambda j, begin=begin: (layer, 0, jnp.clip(j - begin, 0, per - 1))))
        out_specs.append(pl.BlockSpec(memory_space=pl.ANY))
        out_shape.append(jax.ShapeDtypeStruct((tokens, d), F32))
        scratch += [pltpu.VMEM((tokens, d), F32), pltpu.SemaphoreType.DMA]
    return pl.pallas_call(
        functools.partial(gradient_kernel, n_c, per, with_da),
        grid=(n_c + STAGES * LAG,),
        in_specs=in_specs,
        out_specs=out_specs,
        out_shape=out_shape,
        scratch_shapes=scratch,
        compiler_params=params(collective_id=collective_id, has_side_effects=True),
        cost_estimate=pl.CostEstimate(
            flops=(5 if with_da else 3) * 2 * tokens * d * ff, bytes_accessed=2 * (w * tokens * ff + 2 * d * tokens), transcendentals=0
        ),
        name="gradients_da" if with_da else "gradients",
    )(at.reshape(2, 2, d // 2, tokens), b, *(weights or ()))


def adamw(w, m, v, g):
    m = 0.9 * m + 0.1 * g
    v = 0.95 * v + 0.05 * g * g
    step = m * lax.rsqrt(v + 1e-8) + 0.1 * w
    return (w - 0.02 * step).astype(BF16), m, v


def adamw_kernel(first, turn, g_ref, w_ref, m_ref, v_ref, *refs):
    w_out, m_out, v_out = refs[-3:]
    color = lax.rem(pl.program_id(0) + first, len(ORDERS))
    rows = g_ref.shape[2]
    by_order = [owners(o) for o in ORDERS]

    def block(p):
        return g_ref[pick(color, [o[p] for o in by_order]), 0].astype(F32)

    together = 128 // rows if turn else 1
    for p in range(0, GROUP, together):
        g = block(p) if not turn else jnp.concatenate([block(p + i) for i in range(together)], 0).T
        at = slice(p * rows, (p + together) * rows)
        at = (0, slice(None), at) if turn else (0, at)
        w_out[at], m_out[at], v_out[at] = adamw(w_ref[at].astype(F32), m_ref[at], v_ref[at], g)


def update(g, which, first, turn, w, m, v, layer, so_far):
    _, d, ff = w.shape if not turn else (w.shape[0], w.shape[2], w.shape[1])
    rows = g.shape[2]
    spec = pl.BlockSpec((1, CHUNK, d), lambda j: (layer, j, 0)) if turn else pl.BlockSpec((1, d, CHUNK), lambda j: (layer, 0, j))
    more = () if so_far is None else so_far
    return pl.pallas_call(
        functools.partial(adamw_kernel, first, turn),
        grid=(ff // CHUNK,),
        in_specs=[pl.BlockSpec((GROUP, 1, rows, CHUNK), lambda j: (0, which, 0, j)), spec, spec, spec]
        + [pl.BlockSpec(memory_space=pl.ANY)] * len(more),
        out_specs=[spec] * 3,
        out_shape=[jax.ShapeDtypeStruct(w.shape, BF16), jax.ShapeDtypeStruct(w.shape, F32), jax.ShapeDtypeStruct(w.shape, F32)],
        input_output_aliases={4 + i: i for i in range(len(more))},
        compiler_params=params(),
        cost_estimate=pl.CostEstimate(flops=d * ff * 1500, bytes_accessed=22 * d * ff, transcendentals=d * ff),
        name="adamw_turned" if turn else "adamw",
    )(g, w, m, v, *more)


def solution(mesh):
    def step(x, dy, *arrays):
        weights, m, v = (arrays[i : i + 3] for i in (0, 3, 6))
        w_gate, w_up, w_down = weights
        x, dy = x[0], dy[0]
        per = w_gate.shape[2] // CHUNK

        gate, up, mid = forward(x, w_gate, w_up, 0)
        h = down(mid, w_down, x, 0)
        b, at = backward_mid(h, dy, 1, w_down, weights=(w_gate, w_up))
        part, by_a = gradients(at, b, 1, 1, weights=(w_gate, w_up))
        g_1 = lax.all_gather(part, "dp", axis=0)
        by_h = dy + jax.vjp(normed, h)[1](by_a.astype(BF16))[0]
        b, at = backward_mid(x, by_h, 0, w_down, kept=(gate, up))
        (part,) = gradients(at, b, 2, 0)
        g_0a = lax.all_gather(part[:2], "dp", axis=0)
        g_0b = lax.all_gather(part[2:], "dp", axis=0)
        g_1, part = lax.optimization_barrier((g_1, part))

        order = ((2, 0), (0, 1), (1, 2))
        done = {}
        for i, which in order:
            done[i] = update(g_1, which, which * per, i == 2, weights[i], m[i], v[i], 1, None)
        for i, which in order:
            g, at_g = (g_0a, which) if which < 2 else (g_0b, 0)
            done[i] = update(g, at_g, which * per, i == 2, weights[i], m[i], v[i], 0, done[i])
        return tuple(done[i][which] for which in range(3) for i in range(3))

    return jax.shard_map(
        step,
        mesh=mesh,
        in_specs=(P(("rep", "dp"), None, None),) * 2 + (P(None, None, None),) * 9,
        out_specs=(P("rep", None, None),) * 9,
        check_vma=False,
    )
```

time: 1660 us -> 941 us (0.57)
  Pallas kernels: 0 us -> 880 us
  waiting for transfers between devices: 881 us -> 22.7 us
  matrix products: 522 us -> 0 us
  other arithmetic: 226 us -> 15.4 us
    psum x1 -> x0, waiting for transfers between devices: 881 us -> none  [step(): summed[number] = [lax.psum(by_w[name], 'dp') for name in NAMES]]
    pallas_call x0 -> x12, Pallas kernels: none -> 880 us  [the longest x2 404 us: gradients(): pl.pallas_call(functools.partial(gradient_kernel, n_c, per, with_da), gri...]
    dot_general x15 -> x0, matrix products: 522 us -> none  [the longest x5 190 us: layer(): gate = jnp.dot(a, w['w_gate'], preferred_element_type=jnp.float32)]
    convert_element_type x2 -> x0, other arithmetic: 217 us -> none  [adamw(): return ((w - 0.02 * step).astype(jnp.bfloat16), m, v)]
    all_gather x0 -> x3, waiting for transfers between devices: none -> 22.6 us  [the longest x1 13.4 us: step(): g_0a = lax.all_gather(part[:2], 'dp', axis=0)]
  transfers between devices with their start and end apart: 1 -> 3, of which waited for: 1 -> 2; matrix products, arithmetic and copies ran while one was open for 0% -> 2% of each run, Pallas kernels for 0% -> 51%
where the time goes in v1:
time: 941 us; the launch traced here: 936 us
  Pallas kernels  880 us (94%)
  waiting for transfers between devices  22.7 us (2%)
  other arithmetic  15.4 us (2%)
  between operations  14 us (1%)
    pallas_call x2, Pallas kernels, gradients(): pl.pallas_call(functools.partial(gradient_kernel, n_c, per, with_da), gri...  404 us
    pallas_call x6, Pallas kernels, update(): pl.pallas_call(functools.partial(adamw_kernel, first, turn), grid=(ff //...  234 us
    pallas_call x2, Pallas kernels, backward_mid(): pl.pallas_call(functools.partial(last_kernel if kept is None else middle_...  160 us
    pallas_call x1, Pallas kernels, forward(): pl.pallas_call(functools.partial(forward_kernel, 4), grid=(ff // CHUNK,),...  53.8 us
    pallas_call x1, Pallas kernels, down(): pl.pallas_call(down_kernel, grid=(tokens // rows,), in_specs=[pl.BlockSpe...  29.7 us
  transfers between devices with their start and end apart: 3, of which 2 were waited for; matrix products, arithmetic and copies ran while one was open for 2% of the time, Pallas kernels for 51%

profile of v1, /device:TPU:0, one launch (start us, length us, event | category | flops | bytes accessed | tf_op | source)
XLA Modules:
  0.0 936.3 jit_solution(4684563182638927516)
XLA Ops:
  7.2 0.0 all-gather.9.cloned.1.call-start
  7.2 53.8 %forward.1 = (f32[2048,5120]{1,0:T(8,128)}, f32[2048,5120]{1,0:T(8,128)}, bf16[2048,5120]{1,0:T(8,128)(2,1)}) custom-call(bf16[2048,1024]{1,0:T(8,128)(2,1)} %bitcast.14, bf16[2,1024,5120]{2,1,0:T(8,128)(2,1)} %w_ref.9, bf16[2,1024,5120]{2,1,0:T(8,128)(2,1)} %w_ref.11), custom_call_target="tpu_custom_call" | custom-call | flops 42949672960 | bytes 104857600 | tf_op jit(solution)/shard_map/forward/pallas_call | solution.py:92
  61.1 29.7 %down.1.h_ref = bf16[2048,1024]{1,0:T(8,128)(2,1)} custom-call(bf16[2048,5120]{1,0:T(8,128)(2,1)} %get-tuple-element.37.mid_ref, bf16[2,5120,1024]{2,1,0:T(8,128)(2,1)} %w_ref.13, bf16[2048,1024]{1,0:T(8,128)(2,1)} %bitcast.15), custom_call_target="tpu_custom_call" | custom-call | flops 21474836480 | bytes 31457280 | tf_op jit(solution)/shard_map/down/pallas_call | solution.py:113
  90.7 90.1 %last.1 = (bf16[3,2048,5120]{2,1,0:T(8,128)(2,1)}, bf16[2,1024,2048]{2,1,0:T(8,128)(2,1)}) custom-call(bf16[2048,1024]{1,0:T(8,128)(2,1)} %down.1.h_ref, bf16[2048,1024]{1,0:T(8,128)(2,1)} %bitcast.17, bf16[2,1024,5120]{2,1,0:T(8,128)(2,1)} %w_ref.9, bf16[2,1024,5120]{2,1,0:T(8,128)(2,1)} %w_ref.11, bf16[2,5120,1024]{2,1,0:T(8,128)(2,1)} %w_ref.13), custom_call_target="tpu_custom_call" | custom-call | flops 64424509440 | bytes 146800640 | tf_op jit(solution)/shard_map/last/pallas_call | solution.py:190
  180.8 188.1 %gradients_da.1 = (bf16[3,32,5120]{2,1,0:T(8,128)(2,1)}, f32[2048,1024]{1,0:T(8,128)}) custom-call(bf16[2,2,512,2048]{3,2,1,0:T(8,128)(2,1)} %bitcast.19, bf16[3,2048,5120]{2,1,0:T(8,128)(2,1)} %get-tuple-element.39.refs_1_, bf16[2,1024,5120]{2,1,0:T(8,128)(2,1)} %w_ref.9, bf16[2,1024,5120]{2,1,0:T(8,128)(2,1)} %w_ref.11), custom_call_target="tpu_custom_call" | custom-call | flops 107374182400 | bytes 71303168 | tf_op jit(solution)/shard_map/gradients_da/pallas_call | solution.py:332
  368.9 0.0 all-gather.9.cloned.1.call-update
  368.9 0.0 all-gather.7.cloned.1.call-start
  368.9 6.3 fusion.2
  375.3 9.1 fusion.4.dy_ref
  384.3 69.7 %middle.1 = (bf16[3,2048,5120]{2,1,0:T(8,128)(2,1)}, bf16[2,1024,2048]{2,1,0:T(8,128)(2,1)}) custom-call(bf16[2048,1024]{1,0:T(8,128)(2,1)} %bitcast.16, bf16[2048,1024]{1,0:T(8,128)(2,1)} %fusion.4.dy_ref, f32[2048,5120]{1,0:T(8,128)} %get-tuple-element.41.gate_ref, f32[2048,5120]{1,0:T(8,128)} %get-tuple-element.42.up_ref, bf16[2,5120,1024]{2,1,0:T(8,128)(2,1)} %w_ref.13), custom_call_target="tpu_custom_call" | custom-call | flops 21474836480 | bytes 146800640 | tf_op jit(solution)/shard_map/middle/pallas_call | solution.py:190
  454.1 215.5 %gradients.1 = bf16[3,32,5120]{2,1,0:T(8,128)(2,1)} custom-call(bf16[2,2,512,2048]{3,2,1,0:T(8,128)(2,1)} %bitcast.18, bf16[3,2048,5120]{2,1,0:T(8,128)(2,1)} %get-tuple-element.44.refs_1_), custom_call_target="tpu_custom_call" | custom-call | flops 64424509440 | bytes 71303168 | tf_op jit(solution)/shard_map/gradients/pallas_call | solution.py:332
  669.6 2.0 slice.6
  671.5 0.0 all-gather.7.cloned.1.call-update
  671.6 0.0 all-gather.11.cloned.1.call-start
  671.6 1.7 slice.7
  673.3 0.0 all-gather.11.cloned.1.call-update
  673.4 0.0 all-gather.9.cloned.1.call-done
  673.4 40.0 %adamw_turned.2 = (bf16[2,5120,1024]{2,1,0:T(8,128)(2,1)}, f32[2,5120,1024]{2,1,0:T(8,128)}, f32[2,5120,1024]{2,1,0:T(8,128)}) custom-call(bf16[32,3,32,5120]{3,2,1,0:T(8,128)(2,1)} %bitcast.8, bf16[2,5120,1024]{2,1,0:T(8,128)(2,1)} %w_ref.13, f32[2,5120,1024]{2,1,0:T(8,128)} %m_ref.11, f32[2,5120,1024]{2,1,0:T(8,128)} %v_ref.11), custom_call_target="tpu_custom_call" | custom-call | flops 7864320000 | bytes 115343360 | tf_op jit(solution)/shard_map/adamw_turned/pallas_call | solution.py:376
  713.4 38.5 %adamw.6 = (bf16[2,1024,5120]{2,1,0:T(8,128)(2,1)}, f32[2,1024,5120]{2,1,0:T(8,128)}, f32[2,1024,5120]{2,1,0:T(8,128)}) custom-call(bf16[32,3,32,5120]{3,2,1,0:T(8,128)(2,1)} %bitcast.9, bf16[2,1024,5120]{2,1,0:T(8,128)(2,1)} %w_ref.11, f32[2,1024,5120]{2,1,0:T(8,128)} %m_ref.9, f32[2,1024,5120]{2,1,0:T(8,128)} %v_ref.9), custom_call_target="tpu_custom_call" | custom-call | flops 7864320000 | bytes 115343360 | tf_op jit(solution)/shard_map/adamw/pallas_call | solution.py:376
  751.9 38.5 %adamw.4 = (bf16[2,1024,5120]{2,1,0:T(8,128)(2,1)}, f32[2,1024,5120]{2,1,0:T(8,128)}, f32[2,1024,5120]{2,1,0:T(8,128)}) custom-call(bf16[32,3,32,5120]{3,2,1,0:T(8,128)(2,1)} %bitcast.10, bf16[2,1024,5120]{2,1,0:T(8,128)(2,1)} %w_ref.9, f32[2,1024,5120]{2,1,0:T(8,128)} %m_ref.7, f32[2,1024,5120]{2,1,0:T(8,128)} %v_ref.7), custom_call_target="tpu_custom_call" | custom-call | flops 7864320000 | bytes 115343360 | tf_op jit(solution)/shard_map/adamw/pallas_call | solution.py:376
  790.4 13.4 %all-gather.7.cloned.1.call-done = bf16[64,32,5120]{2,1,0:T(8,128)(2,1)} async-done(((bf16[2,32,5120]{2,1,0:T(8,128)(2,1)}), bf16[64,32,5120]{2,1,0:T(8,128)(2,1)}) %all-gather.7.cloned.1.call-update) | async-done | bytes 20971536 | tf_op jit(solution)/shard_map/all_gather | solution.py:405
  803.9 39.8 %adamw_turned.3 = (bf16[2,5120,1024]{2,1,0:T(8,128)(2,1)}, f32[2,5120,1024]{2,1,0:T(8,128)}, f32[2,5120,1024]{2,1,0:T(8,128)}) custom-call(bf16[32,2,32,5120]{3,2,1,0:T(8,128)(2,1)} %bitcast.11, bf16[2,5120,1024]{2,1,0:T(8,128)(2,1)} %w_ref.13, f32[2,5120,1024]{2,1,0:T(8,128)} %m_ref.11, ...), custom_call_target="tpu_custom_call", output_to_operand_aliasing={{0}: (4, {}), {1}: (5, {}), {2}: (6, {})} | custom-call | flops 7864320000 | bytes 115343360 | tf_op jit(solution)/shard_map/adamw_turned/pallas_call | solution.py:376
  843.7 38.4 %adamw.5 = (bf16[2,1024,5120]{2,1,0:T(8,128)(2,1)}, f32[2,1024,5120]{2,1,0:T(8,128)}, f32[2,1024,5120]{2,1,0:T(8,128)}) custom-call(bf16[32,2,32,5120]{3,2,1,0:T(8,128)(2,1)} %bitcast.12, bf16[2,1024,5120]{2,1,0:T(8,128)(2,1)} %w_ref.9, f32[2,1024,5120]{2,1,0:T(8,128)} %m_ref.7, ...), custom_call_target="tpu_custom_call", output_to_operand_aliasing={{0}: (4, {}), {1}: (5, {}), {2}: (6, {})} | custom-call | flops 7864320000 | bytes 115343360 | tf_op jit(solution)/shard_map/adamw/pallas_call | solution.py:376
  882.1 9.2 all-gather.11.cloned.1.call-done
  891.2 38.3 %adamw.7 = (bf16[2,1024,5120]{2,1,0:T(8,128)(2,1)}, f32[2,1024,5120]{2,1,0:T(8,128)}, f32[2,1024,5120]{2,1,0:T(8,128)}) custom-call(bf16[32,1,32,5120]{3,2,1,0:T(8,128)(2,1)} %bitcast.13, bf16[2,1024,5120]{2,1,0:T(8,128)(2,1)} %w_ref.11, f32[2,1024,5120]{2,1,0:T(8,128)} %m_ref.9, ...), custom_call_target="tpu_custom_call", output_to_operand_aliasing={{0}: (4, {}), {1}: (5, {}), {2}: (6, {})} | custom-call | flops 7864320000 | bytes 115343360 | tf_op jit(solution)/shard_map/adamw/pallas_call | solution.py:376
  (1 shorter events, 0.0 us)
Async XLA Ops:
  7.2 666.2 %all-gather.9.cloned.1.call-start = ((), (), s32[]{:S(2)}) async-start(), calls=%async_computation.1 | async-start | bytes 32440320 | tf_op jit(solution)/shard_map/all_gather | solution.py:401
  368.9 435.0 %all-gather.7.cloned.1.call-start = ((), (), s32[]{:S(2)}) async-start(), calls=%async_computation | async-start | bytes 21626880 | tf_op jit(solution)/shard_map/all_gather | solution.py:405
  671.6 219.7 %all-gather.11.cloned.1.call-start = ((), (), s32[]{:S(2)}) async-start(), calls=%async_computation.2 | async-start | bytes 10813440 | tf_op jit(solution)/shard_map/all_gather | solution.py:406
Sparse Core Ops, SparseCore 0:
  369.0 231.5 all-gather.8
  671.7 132.1 all-gather.6
  806.8 84.4 all-gather.10

commit v2 on v0

v2 whole, which is shorter than its diff:
```python
import functools

import jax
import jax.numpy as jnp
from jax import lax
from jax.experimental import pallas as pl
from jax.experimental.pallas import tpu as pltpu
from jax.sharding import PartitionSpec as P

MESH = pl.DeviceIdType.MESH
F32, BF16 = jnp.float32, jnp.bfloat16
MIB = 1024 * 1024

CORE, Z0, Z1, Y, X = 1, 2, 4, 8, 16
BITS = (CORE, Z0, Z1, Y, X)
ORDERS = (
    ((CORE, X, Y, Z0, Z1),) * 2,
    ((CORE, Y, X, Z0, Z1),) * 2,
    ((CORE, Z0, X, Y, Z1), (CORE, Z0, Y, X, Z1)),
)
STAGES = 5
GROUP = 1 << STAGES
CHUNK = 512
EARLY = 5
WAIT = 2


def position(order, device):
    return sum(((device // m) % 2) << (STAGES - 1 - i) for i, m in enumerate(order))


def owners(order):
    found = [0] * GROUP
    for device in range(GROUP):
        found[position(order, device)] = device
    return found


def params(limit=61, **more):
    return pltpu.CompilerParams(dimension_semantics=("arbitrary",), vmem_limit_bytes=limit * MIB, **more)


def dot(a, b):
    return jnp.dot(a, b, preferred_element_type=F32)


def dot_nt(a, b):
    return lax.dot_general(a, b, (((1,), (1,)), ((), ())), preferred_element_type=F32)


def once(shape, index):
    return pl.BlockSpec(shape, index, pipeline_mode=pl.Buffered(1))


def norm_in(h):
    wide = h.astype(F32)
    return (wide * lax.rsqrt(jnp.mean(wide**2, -1, keepdims=True) + 1e-6)).astype(BF16)


def turned(j, out_ref, first_ref, second_ref):
    width = out_ref.shape[1]
    at = pl.ds(pl.multiple_of(lax.rem(j, 4) * width, width), width)

    @pl.when(j < 4)
    def _():
        out_ref[0] = first_ref[:, at].T

    @pl.when((j >= 4) & (j < 8))
    def _():
        out_ref[0] = second_ref[:, at].T


def forward_kernel(parts, h_ref, dy_ref, wg_ref, wu_ref, gate_ref, up_ref, mid_ref, at_ref, a_ref):
    t = h_ref.shape[0] // parts
    j = pl.program_id(0)

    @pl.when(j == 0)
    def _():
        for i in range(parts):
            a_ref[i * t : (i + 1) * t] = norm_in(h_ref[i * t : (i + 1) * t])

    turned(j, at_ref, dy_ref, a_ref)
    for i in range(parts):
        rows = slice(i * t, (i + 1) * t)
        gate = dot(a_ref[rows], wg_ref[0])
        up = dot(a_ref[rows], wu_ref[0])
        gate_ref[rows] = gate
        up_ref[rows] = up
        mid_ref[rows] = (jax.nn.silu(gate) * up).astype(BF16)


def forward(h, dy, w_gate, w_up, layer):
    tokens, d = h.shape
    ff = w_gate.shape[2]
    weight = pl.BlockSpec((1, d, CHUNK), lambda j: (layer, 0, j))
    tile = pl.BlockSpec((tokens, CHUNK), lambda j: (0, j))
    whole = once((tokens, d), lambda j: (0, 0))
    turn = lambda j: (jnp.minimum(j // 4, 1), jnp.where(j < 8, lax.rem(j, 4), 3), 0)
    return pl.pallas_call(
        functools.partial(forward_kernel, 2),
        grid=(ff // CHUNK,),
        in_specs=[whole, whole, weight, weight],
        out_specs=[tile, tile, tile, pl.BlockSpec((1, d // 4, tokens), turn)],
        out_shape=[jax.ShapeDtypeStruct((tokens, ff), t) for t in (F32, F32, BF16)] + [jax.ShapeDtypeStruct((2, d, tokens), BF16)],
        scratch_shapes=[pltpu.VMEM((tokens, d), BF16)],
        compiler_params=params(),
        cost_estimate=pl.CostEstimate(flops=4 * tokens * d * ff, bytes_accessed=10 * tokens * ff, transcendentals=tokens * ff),
        name="forward",
    )(h, dy, w_gate, w_up)


def down_kernel(mid_ref, w_ref, h_ref, out_ref, a_ref, at_ref):
    h = h_ref[...] + dot(mid_ref[...], w_ref[0]).astype(BF16)
    a = norm_in(h)
    out_ref[...] = h
    a_ref[...] = a
    at_ref[...] = a.T


def down(mid, w_down, h, layer):
    tokens, ff = mid.shape
    d = h.shape[1]
    rows = 256
    block = pl.BlockSpec((rows, d), lambda i: (i, 0))
    return pl.pallas_call(
        down_kernel,
        grid=(tokens // rows,),
        in_specs=[pl.BlockSpec((rows, ff), lambda i: (i, 0)), once((1, ff, d), lambda i: (layer, 0, 0)), block],
        out_specs=[block, block, pl.BlockSpec((d, rows), lambda i: (0, i))],
        out_shape=[jax.ShapeDtypeStruct(s, BF16) for s in ((tokens, d), (tokens, d), (d, tokens))],
        compiler_params=params(),
        cost_estimate=pl.CostEstimate(flops=2 * tokens * d * ff, bytes_accessed=2 * (tokens + d) * ff, transcendentals=0),
        name="down",
    )(mid, w_down, h)


class Exchange:
    def __init__(self, n_c, orders, rows):
        self.n_c, self.orders, self.rows = n_c, orders, rows
        self.sizes = [2 ** (STAGES - 1 - s) * rows for s in range(STAGES)]
        self.slots = [2 if orders[0][s] == orders[1][s] else 4 for s in range(STAGES)]

    def scratch(self):
        return (
            [pltpu.VMEM((n, CHUNK), BF16) for n in self.sizes]
            + [pltpu.VMEM((n, CHUNK), F32) for n in self.sizes]
            + [pltpu.VMEM((slots, n, CHUNK), BF16) for n, slots in zip(self.sizes, self.slots, strict=True)]
            + [pltpu.SemaphoreType.DMA((STAGES,)), pltpu.SemaphoreType.DMA((STAGES, max(self.slots)))]
        )

    def bind(self, j, bits, out_ref, refs):
        self.j, self.out_ref = j, out_ref
        self.give, self.keep, self.came = refs[:STAGES], refs[STAGES : 2 * STAGES], refs[2 * STAGES : 3 * STAGES]
        self.send_sem, self.recv_sem = refs[3 * STAGES :]
        self.all_bits = bits

    def bit(self, s, c):
        even, odd = (self.all_bits[order[s]] for order in self.orders)
        return even if self.orders[0][s] == self.orders[1][s] else jnp.where(lax.rem(c, 2) == 0, even, odd)

    def peer(self, s, c):
        me = lax.axis_index("dp")
        even, odd = (me + order[s] * (1 - 2 * self.all_bits[order[s]]) for order in self.orders)
        return even if self.orders[0][s] == self.orders[1][s] else jnp.where(lax.rem(c, 2) == 0, even, odd)

    def copy(self, s, c):
        slot = lax.rem(c, self.slots[s])
        return pltpu.make_async_remote_copy(
            src_ref=self.give[s],
            dst_ref=self.came[s].at[slot],
            send_sem=self.send_sem.at[s],
            recv_sem=self.recv_sem.at[s, slot],
            device_id={"dp": self.peer(s, c)},
            device_id_type=MESH,
        )

    def advance(self):
        for s in reversed(range(STAGES)):
            c = self.j - (s + 1)

            @pl.when((c >= 0) & (c < self.n_c))
            def _(s=s, c=c):
                copy = self.copy(s, c)
                copy.wait_send()
                copy.wait_recv()
                keep, came = self.keep[s], self.came[s].at[lax.rem(c, self.slots[s])]
                if s == STAGES - 1:
                    self.out_ref[...] = (keep[...] + came[...].astype(F32)).astype(BF16)
                else:
                    half = self.sizes[s + 1]
                    bit = self.bit(s + 1, c)
                    theirs = pl.ds(pl.multiple_of((1 - bit) * half, half), half)
                    mine = pl.ds(pl.multiple_of(bit * half, half), half)
                    self.give[s + 1][...] = (keep[theirs] + came[theirs].astype(F32)).astype(BF16)
                    self.copy(s + 1, c).start()
                    self.keep[s + 1][...] = keep[mine] + came[mine].astype(F32)

    def put(self, at_ref, b):
        core = self.bit(0, self.j)
        self.give[0][...] = dot(at_ref[1 - core], b).astype(BF16)
        self.copy(0, self.j).start()
        self.keep[0][...] = dot(at_ref[core], b)


class Gather:
    def __init__(self, n, first, load, begin, rows):
        self.n, self.first, self.load, self.begin, self.rows = n, first, load, begin, rows

    def scratch(self):
        return [
            pltpu.VMEM((self.n, self.rows, CHUNK), BF16),
            pltpu.SemaphoreType.DMA((2,)),
            pltpu.SemaphoreType.DMA((STAGES, 2)),
            pltpu.SemaphoreType.DMA((STAGES, self.n)),
        ]

    def bind(self, ex, part_ref, all_ref, refs):
        self.ex, self.part_ref, self.all_ref = ex, part_ref, all_ref
        self.block, self.own_sem, self.send_sem, self.recv_sem = refs

    def region(self, k, t):
        start = sum(self.ex.bit(i, self.first + t) * 2 ** (STAGES - 1 - i) for i in range(STAGES - k))
        return self.all_ref.at[t, pl.ds(pl.multiple_of(start * self.rows, 2**k * self.rows), 2**k * self.rows)]

    def own(self, t):
        slot = lax.rem(t, 2)
        return pltpu.make_async_copy(self.block.at[t], self.region(0, t), self.own_sem.at[slot])

    def copy(self, k, t):
        slot = lax.rem(t, 2)
        return pltpu.make_async_remote_copy(
            src_ref=self.block.at[t] if k == 0 else self.region(k, t),
            dst_ref=self.region(k, t),
            send_sem=self.send_sem.at[k, slot],
            recv_sem=self.recv_sem.at[k, t],
            device_id={"dp": self.ex.peer(STAGES - 1 - k, self.first + t)},
            device_id_type=MESH,
        )

    def advance(self):
        t = self.ex.j - self.load

        @pl.when((t >= 0) & (t < self.n))
        def _():
            self.block[t] = self.part_ref[...]

        for k in reversed(range(STAGES + 1)):
            t = self.ex.j - self.begin - k

            @pl.when((t >= 0) & (t < self.n))
            def _(k=k, t=t):
                if k > 0:
                    copy = self.copy(k - 1, t)
                    copy.wait_send()
                    copy.wait_recv()
                if k == 1:
                    self.own(t).wait()
                if k == 0:
                    self.own(t).start()
                if k < STAGES:
                    self.copy(k, t).start()


def start_exchanges(exchanges, gathers, step, out_refs, part_refs, all_ref, refs):
    me = lax.axis_index("dp")
    bits = {m: lax.rem(lax.div(me, m), 2) for m in BITS}
    n = len(refs) // len(exchanges)
    for i, (ex, g) in enumerate(zip(exchanges, gathers, strict=True)):
        mine = refs[i * n : (i + 1) * n]
        ex.bind(step, bits, out_refs[i], mine[:-4])
        g.bind(ex, part_refs[i], all_ref.at[i], mine[-4:])

    @pl.when(pl.program_id(0) == 0)
    def _():
        barrier = pltpu.get_barrier_semaphore()
        for m in BITS:
            pl.semaphore_signal(barrier, inc=1, device_id={"dp": me + m * (1 - 2 * bits[m])}, device_id_type=MESH)
        pl.semaphore_wait(barrier, len(BITS))


def through(gate, up, by_mid):
    by_mid = by_mid.astype(BF16).astype(F32)
    s = jax.nn.sigmoid(gate)
    silu = gate * s
    return (silu * up).astype(BF16), (by_mid * up * (s * (1 + gate * (1 - s)))).astype(BF16), (by_mid * silu).astype(BF16)


def norm_back(h, dy, by_a):
    wide, by_a = h.astype(F32), by_a.astype(BF16).astype(F32)
    scale = lax.rsqrt(jnp.mean(wide**2, -1, keepdims=True) + 1e-6)
    by_h = by_a * scale - wide * (scale * scale * scale * jnp.mean(by_a * wide, -1, keepdims=True))
    return dy + by_h.astype(BF16)


def first_kernel(
    exchanges, gathers, parts, dy_ref, dyt_ref, at_ref, gate_ref, up_ref, wd_ref, part_ref, early_ref, late_ref, all_ref, mid_ref, by_gate_ref,
    by_up_ref, *refs
):
    down, gate, up = exchanges
    j = pl.program_id(0)
    outs = [early_ref.at[0], early_ref.at[1], late_ref.at[0]]
    start_exchanges(exchanges, gathers, j, outs, [part_ref.at[i] for i in range(3)], all_ref, refs)
    more = j < down.n_c
    t = dy_ref.shape[0] // parts
    gathers[0].advance()
    down.advance()

    @pl.when(more)
    def _():
        for i in range(parts):
            rows = slice(i * t, (i + 1) * t)
            by_mid = dot_nt(dy_ref[rows], wd_ref[0])
            mid_ref[rows], by_gate_ref[rows], by_up_ref[rows] = through(gate_ref[rows], up_ref[rows], by_mid)

    gathers[1].advance()
    gate.advance()

    @pl.when(more)
    def _():
        down.put(dyt_ref.at[0], mid_ref[...])

    gathers[2].advance()
    up.advance()

    @pl.when(more)
    def _():
        gate.put(at_ref.at[0], by_gate_ref[...])
        up.put(at_ref.at[0], by_up_ref[...])


def last_step(j, n_c):
    return jnp.where(j < n_c, j, n_c + lax.div(j - n_c, 2))


def last_kernel(
    exchanges, gathers, parts, dy_ref, dyt_ref, at_ref, wg_ref, wu_ref, wd_ref, a_ref, h_ref, out_ref, all_ref, by_h_ref, by_ht_ref, b_ref, mid_ref,
    buf_ref, acc_ref, sem, *refs
):
    down, gate, up = exchanges
    n_c = down.n_c
    j = pl.program_id(0)
    t = dy_ref.shape[0] // parts
    i = j - n_c
    take_a = pltpu.make_async_copy(a_ref, buf_ref.at[1], sem.at[0])
    save = lambda c: pltpu.make_async_copy(buf_ref.at[0], b_ref.at[c], sem.at[1])
    fetch = lambda i: pltpu.make_async_copy(b_ref.at[n_c - 1 - i], buf_ref.at[lax.rem(i, 2)], sem.at[2])

    @pl.when(j == 0)
    def _():
        take_a.start()

    step = jnp.where((j < n_c) | (lax.rem(i, 2) == 0), last_step(j, n_c), -GROUP)
    outs = [out_ref.at[i] for i in range(3)]
    start_exchanges(exchanges, gathers, step, outs, outs, all_ref, refs)

    @pl.when(j == 0)
    def _():
        take_a.wait()

    @pl.when((j >= 1) & (j <= n_c))
    def _():
        save(j - 1).wait()

    for ex, g in zip(exchanges, gathers, strict=True):
        ex.advance()
        g.advance()

    @pl.when(j < n_c)
    def _():
        for p in range(parts):
            rows = slice(p * t, (p + 1) * t)
            by_mid = dot_nt(dy_ref[rows], wd_ref[0])
            a = buf_ref[1, rows]
            mid_ref[rows], buf_ref[0, rows, :CHUNK], buf_ref[0, rows, CHUNK:] = through(dot(a, wg_ref[0]), dot(a, wu_ref[0]), by_mid)
        save(j).start()
        down.put(dyt_ref.at[0], mid_ref[...])
        gate.put(at_ref.at[0], buf_ref[0, :, :CHUNK])
        up.put(at_ref.at[0], buf_ref[0, :, CHUNK:])

    @pl.when((i >= 0) & (i < n_c))
    def _():
        @pl.when(i >= 1)
        def _():
            fetch(i).wait()

        @pl.when(i < n_c - 1)
        def _():
            fetch(i + 1).start()

        slot = lax.rem(i, 2)
        for p in range(parts):
            rows = slice(p * t, (p + 1) * t)
            term = dot_nt(buf_ref[slot, rows, :CHUNK], wg_ref[0]) + dot_nt(buf_ref[slot, rows, CHUNK:], wu_ref[0])

            @pl.when(i == 0)
            def _():
                acc_ref[rows] = term

            @pl.when(i > 0)
            def _():
                acc_ref[rows] += term

    n = by_h_ref.shape[0]
    block = i - n_c

    @pl.when(block >= 0)
    def _():
        rows = pl.ds(pl.multiple_of(block * n, n), n)
        by_h = norm_back(h_ref[...], dy_ref[rows], acc_ref[rows])
        by_h_ref[...] = by_h
        by_ht_ref[...] = by_h.T


def piece(at, which):
    n, d, tokens = at.shape
    return once((1, 2, d // 2, tokens), lambda j: (which, 0, 0, 0)), at.reshape(n, 2, d // 2, tokens)


def backward(layer, w_down, collective_id, dy, dy_t, a_t, kept=None, part=None, a=None, h=None, weights=None):
    tokens, d = dy.shape
    ff = w_down.shape[1]
    n_c, rows = ff // CHUNK, d // GROUP
    exchanges = [Exchange(n_c, orders, rows) for orders in ORDERS]
    chunks, first, load, begin = (EARLY, 0, STAGES, STAGES + WAIT) if kept is None else (n_c - EARLY, EARLY, 0, 0)
    gathers = [Gather(chunks, first, load, begin, rows) for _ in ORDERS]
    clip = lambda j: jnp.minimum(j, n_c - 1)
    dyt_spec, dy_t = piece(*dy_t)
    at_spec, a_t = piece(*a_t)
    tile = pl.BlockSpec((tokens, CHUNK), lambda j: (0, clip(j)))
    weight = pl.BlockSpec((1, d, CHUNK), lambda j: (layer, 0, jnp.where(j < n_c, j, jnp.maximum(2 * n_c - 1 - j, 0))))
    specs = [once((tokens, d), lambda j: (0, 0)), dyt_spec, at_spec] + ([tile, tile] if kept is not None else [weight, weight])
    specs.append(pl.BlockSpec((1, CHUNK, d), lambda j: (layer, clip(j), 0)))
    args = [dy, dy_t, a_t, *(kept if kept is not None else weights), w_down]
    step = (lambda j: j) if kept is not None else (lambda j: last_step(j, n_c))
    parts = (2, 1) if kept is not None else (3,)
    out_specs = [pl.BlockSpec((n, rows, CHUNK), lambda j: (0, 0, jnp.clip(step(j) - STAGES, 0, n_c - 1))) for n in parts]
    out_specs.append(pl.BlockSpec(memory_space=pl.ANY))
    out_shape = [jax.ShapeDtypeStruct((n, rows, ff), BF16) for n in parts] + [jax.ShapeDtypeStruct((3, chunks, d, CHUNK), BF16)]
    scratch = [pltpu.VMEM((tokens, CHUNK), BF16)]
    if kept is not None:
        specs.append(pl.BlockSpec((3, rows, CHUNK), lambda j: (0, 0, EARLY + jnp.minimum(j, chunks - 1))))
        args.append(part)
        scratch += scratch * 2
        grid = n_c + STAGES
    else:
        n = 256
        grid = 2 * n_c + tokens // n
        block = lambda j: jnp.maximum(j - 2 * n_c, 0)
        specs += [pl.BlockSpec(memory_space=pl.ANY), pl.BlockSpec((n, d), lambda j: (block(j), 0))]
        args += [a, h]
        out_specs += [pl.BlockSpec((n, d), lambda j: (block(j), 0)), pl.BlockSpec((d, n), lambda j: (0, block(j)))]
        out_specs.append(pl.BlockSpec(memory_space=pl.ANY))
        out_shape += [jax.ShapeDtypeStruct((tokens, d), BF16), jax.ShapeDtypeStruct((d, tokens), BF16)]
        out_shape.append(jax.ShapeDtypeStruct((n_c, tokens, 2 * CHUNK), BF16))
        scratch += [pltpu.VMEM((2, tokens, d), BF16), pltpu.VMEM((tokens, d), F32), pltpu.SemaphoreType.DMA((3,))]
    return pl.pallas_call(
        functools.partial(first_kernel if kept is not None else last_kernel, exchanges, gathers, 4 if kept is not None else 2),
        grid=(grid,),
        in_specs=specs,
        out_specs=out_specs,
        out_shape=out_shape,
        scratch_shapes=scratch + [one for ex, g in zip(exchanges, gathers, strict=True) for one in ex.scratch() + g.scratch()],
        compiler_params=params(collective_id=collective_id, has_side_effects=True),
        cost_estimate=pl.CostEstimate(
            flops=(8 if kept is not None else 16) * tokens * d * ff, bytes_accessed=8 * tokens * ff, transcendentals=tokens * ff
        ),
        name="first" if kept is not None else "last",
    )(*args)


def adamw(w, m, v, g):
    m = 0.9 * m + 0.1 * g
    v = 0.95 * v + 0.05 * g * g
    step = m * lax.rsqrt(v + 1e-8) + 0.1 * w
    return (w - 0.02 * step).astype(BF16), m, v


def adamw_kernel(orders, turn, *refs):
    (w_ref, m_ref, v_ref), (w_out, m_out, v_out) = refs[:3], refs[-3:]
    g_refs = refs[3:5] if orders is None else refs[3:4]
    rows = 128
    for p in range(m_ref.shape[2 if turn else 1] // rows):
        at = slice(p * rows, (p + 1) * rows)
        if orders is None:
            early = pl.program_id(0) < EARLY
            g = jnp.where(early, g_refs[0][0, 0, at], g_refs[1][0, 0, at]).astype(F32)
        else:
            n = g_refs[0].shape[2]
            even, odd = (owners(order)[p * rows // n : (p + 1) * rows // n] for order in orders)
            device = lambda a, b: a if a == b else jnp.where(lax.rem(pl.program_id(0), 2) == 0, a, b)
            g = jnp.concatenate([g_refs[0][device(a, b), 0].astype(F32) for a, b in zip(even, odd, strict=True)], 0)
        at = (0, slice(None), at) if turn else (0, at)
        w_out[at], m_out[at], v_out[at] = adamw(w_ref[at].astype(F32), m_ref[at], v_ref[at], g.T if turn else g)


def update(g, which, matrix, w, m, v, layer, so_far):
    turn = matrix == 0
    _, d, ff = w.shape if not turn else (w.shape[0], w.shape[2], w.shape[1])
    spec = pl.BlockSpec((1, CHUNK, d), lambda j: (layer, j, 0)) if turn else pl.BlockSpec((1, d, CHUNK), lambda j: (layer, 0, j))
    more = () if so_far is None else so_far
    if len(g) == 2:
        g_specs = [
            pl.BlockSpec((1, 1, d, CHUNK), lambda j: (which, jnp.minimum(j, EARLY - 1), 0, 0)),
            pl.BlockSpec((1, 1, d, CHUNK), lambda j: (which, jnp.maximum(j - EARLY, 0), 0, 0)),
        ]
    else:
        g_specs = [pl.BlockSpec((GROUP, 1, g[0].shape[2], CHUNK), lambda j: (0, which, 0, j))]
    return pl.pallas_call(
        functools.partial(adamw_kernel, None if len(g) == 2 else ORDERS[matrix], turn),
        grid=(ff // CHUNK,),
        in_specs=[spec, spec, spec] + g_specs + [pl.BlockSpec(memory_space=pl.ANY)] * len(more),
        out_specs=[spec] * 3,
        out_shape=[jax.ShapeDtypeStruct(w.shape, BF16), jax.ShapeDtypeStruct(w.shape, F32), jax.ShapeDtypeStruct(w.shape, F32)],
        input_output_aliases={3 + len(g) + i: i for i in range(len(more))},
        compiler_params=params(),
        cost_estimate=pl.CostEstimate(flops=d * ff * 1500, bytes_accessed=22 * d * ff, transcendentals=d * ff),
        name="adamw_turned" if turn else "adamw",
    )(w, m, v, *g, *more)


def solution(mesh):
    def step(x, dy, *arrays):
        weights, m, v = (arrays[i : i + 3] for i in (0, 3, 6))
        w_gate, w_up, w_down = weights
        x, dy = x[0], dy[0]

        gate, up, mid, at = forward(x, dy, w_gate, w_up, 0)
        h, a, a_t = down(mid, w_down, x, 0)
        part, g_1a, by_h, by_h_t, _ = backward(1, w_down, 1, dy, (at, 0), (a_t[None], 0), a=a, h=h, weights=(w_gate, w_up))
        early, late, g_1b = backward(0, w_down, 2, by_h, (by_h_t[None], 0), (at, 1), kept=(gate, up), part=part)
        g_0a = lax.all_gather(early, "dp", axis=0)
        g_0b = lax.all_gather(late, "dp", axis=0)

        place = (2, 0, 1)
        new = {i: update((g_1a, g_1b), i, i, weights[place[i]], m[place[i]], v[place[i]], 1, None) for i in range(3)}
        g_0a, *_ = lax.optimization_barrier((g_0a, *new.values()))
        for i in range(3):
            g, which = (g_0a, i) if i < 2 else (g_0b, 0)
            if i == 2:
                g, new[0], new[1] = lax.optimization_barrier((g, new[0], new[1]))
            new[i] = update((g,), which, i, weights[place[i]], m[place[i]], v[place[i]], 0, new[i])
        return tuple(new[i][which] for which in range(3) for i in (1, 2, 0))

    return jax.shard_map(
        step,
        mesh=mesh,
        in_specs=(P(("rep", "dp"), None, None),) * 2 + (P(None, None, None),) * 9,
        out_specs=(P("rep", None, None),) * 9,
        check_vma=False,
    )
```

time: 1660 us -> 818 us (0.49)
  waiting for transfers between devices: 881 us -> 22.8 us
  Pallas kernels: 0 us -> 775 us
  matrix products: 522 us -> 0 us
  other arithmetic: 226 us -> 0 us
    psum x1 -> x0, waiting for transfers between devices: 881 us -> none  [step(): summed[number] = [lax.psum(by_w[name], 'dp') for name in NAMES]]
    pallas_call x0 -> x10, Pallas kernels: none -> 775 us  [the longest x2 451 us: backward(): pl.pallas_call(functools.partial(first_kernel if kept is not None else la...]
    dot_general x15 -> x0, matrix products: 522 us -> none  [the longest x5 190 us: layer(): gate = jnp.dot(a, w['w_gate'], preferred_element_type=jnp.float32)]
    convert_element_type x2 -> x0, other arithmetic: 217 us -> none  [adamw(): return ((w - 0.02 * step).astype(jnp.bfloat16), m, v)]
    all_gather x0 -> x2, waiting for transfers between devices: none -> 22.1 us  [the longest x1 12.4 us: step(): g_0a = lax.all_gather(early, 'dp', axis=0)]
  transfers between devices with their start and end apart: 1 -> 2, of which waited for: 1 -> 2; matrix products, arithmetic and copies ran while one was open for 0% -> 0% of each run, Pallas kernels for 0% -> 24%
where the time goes in v2:
time: 818 us; the launch traced here: 812 us
  Pallas kernels  775 us (95%)
  waiting for transfers between devices  22.8 us (3%)
  between operations  14.5 us (2%)
    pallas_call x2, Pallas kernels, backward(): pl.pallas_call(functools.partial(first_kernel if kept is not None else la...  451 us
    pallas_call x6, Pallas kernels, update(): pl.pallas_call(functools.partial(adamw_kernel, None if len(g) == 2 else O...  235 us
    pallas_call x1, Pallas kernels, forward(): pl.pallas_call(functools.partial(forward_kernel, 2), grid=(ff // CHUNK,),...  57.4 us
    pallas_call x1, Pallas kernels, down(): pl.pallas_call(down_kernel, grid=(tokens // rows,), in_specs=[pl.BlockSpe...  31.8 us
  transfers between devices with their start and end apart: 2, of which 2 were waited for; matrix products, arithmetic and copies ran while one was open for 0% of the time, Pallas kernels for 24%

profile of v2, /device:TPU:0, one launch (start us, length us, event | category | flops | bytes accessed | tf_op | source)
XLA Modules:
  0.0 812.0 jit_solution(15615680046760817409)
XLA Ops:
  7.2 0.0 all-gather.7.cloned.1.call-start
  7.2 57.4 %forward.1 = (f32[2048,5120]{1,0:T(8,128)}, f32[2048,5120]{1,0:T(8,128)}, bf16[2048,5120]{1,0:T(8,128)(2,1)}, bf16[2,1024,2048]{2,1,0:T(8,128)(2,1)}) custom-call(bf16[2048,1024]{1,0:T(8,128)(2,1)} %bitcast.10, bf16[2048,1024]{1,0:T(8,128)(2,1)} %bitcast.12, bf16[2,1024,5120]{2,1,0:T(8,128)(2,1)} %refs_0_.10, bf16[2,1024,5120]{2,1,0:T(8,128)(2,1)} %refs_0_.11), custom_call_target="tpu_custom_call" | custom-call | flops 42949672960 | bytes 104857600 | tf_op jit(solution)/shard_map/forward/pallas_call | solution.py:99
  64.7 31.8 %down.1 = (bf16[2048,1024]{1,0:T(8,128)(2,1)}, bf16[2048,1024]{1,0:T(8,128)(2,1)}, bf16[1024,2048]{1,0:T(8,128)(2,1)}) custom-call(bf16[2048,5120]{1,0:T(8,128)(2,1)} %get-tuple-element.50.mid_ref, bf16[2,5120,1024]{2,1,0:T(8,128)(2,1)} %refs_0_.9, bf16[2048,1024]{1,0:T(8,128)(2,1)} %bitcast.11), custom_call_target="tpu_custom_call" | custom-call | flops 21474836480 | bytes 31457280 | tf_op jit(solution)/shard_map/down/pallas_call | solution.py:125
  96.5 248.9 %last.1 = (bf16[3,32,5120]{2,1,0:T(8,128)(2,1)}, bf16[3,5,1024,512]{3,2,1,0:T(8,128)(2,1)}, bf16[2048,1024]{1,0:T(8,128)(2,1)}, bf16[1024,2048]{1,0:T(8,128)(2,1)}, bf16[10,2048,1024]{2,1,0:T(8,128)(2,1)}) custom-call(bf16[2048,1024]{1,0:T(8,128)(2,1)} %bitcast.13, bf16[2,2,512,2048]{3,2,1,0:T(8,128)(2,1)} %bitcast.14, bf16[1,2,512,2048]{3,2,1,0:T(8,128)(2,1)} %bitcast.17, ...), custom_call_target="tpu_custom_call" | custom-call | flops 171798691840 | bytes 83886080 | tf_op jit(solution)/shard_map/last/pallas_call | solution.py:456
  345.4 201.8 %first.1 = (bf16[2,32,5120]{2,1,0:T(8,128)(2,1)}, bf16[1,32,5120]{2,1,0:T(8,128)(2,1)}, bf16[3,5,1024,512]{3,2,1,0:T(8,128)(2,1)}) custom-call(bf16[2048,1024]{1,0:T(8,128)(2,1)} %get-tuple-element.54.dy_ref, bf16[1,2,512,2048]{3,2,1,0:T(8,128)(2,1)} %bitcast.16, bf16[2,2,512,2048]{3,2,1,0:T(8,128)(2,1)} %bitcast.15, ...), custom_call_target="tpu_custom_call" | custom-call | flops 85899345920 | bytes 83886080 | tf_op jit(solution)/shard_map/first/pallas_call | solution.py:456
  547.2 0.0 all-gather.7.cloned.1.call-update
  547.2 0.0 all-gather.5.cloned.1.call-start
  547.3 0.7 all-gather.5.cloned.1.call-update
  548.0 39.6 %adamw.5 = (bf16[2,1024,5120]{2,1,0:T(8,128)(2,1)}, f32[2,1024,5120]{2,1,0:T(8,128)}, f32[2,1024,5120]{2,1,0:T(8,128)}) custom-call(bf16[2,1024,5120]{2,1,0:T(8,128)(2,1)} %refs_0_.11, f32[2,1024,5120]{2,1,0:T(8,128)} %refs_1_.11, f32[2,1024,5120]{2,1,0:T(8,128)} %refs_2_.11, bf16[3,5,1024,512]{3,2,1,0:T(8,128)(2,1)} %get-tuple-element.61.refs_3_, ...), custom_call_target="tpu_custom_call" | custom-call | flops 7864320000 | bytes 115343360 | tf_op jit(solution)/shard_map/adamw/pallas_call | solution.py:508
  587.6 39.3 %adamw.4 = (bf16[2,1024,5120]{2,1,0:T(8,128)(2,1)}, f32[2,1024,5120]{2,1,0:T(8,128)}, f32[2,1024,5120]{2,1,0:T(8,128)}) custom-call(bf16[2,1024,5120]{2,1,0:T(8,128)(2,1)} %refs_0_.10, f32[2,1024,5120]{2,1,0:T(8,128)} %refs_1_.10, f32[2,1024,5120]{2,1,0:T(8,128)} %refs_2_.10, bf16[3,5,1024,512]{3,2,1,0:T(8,128)(2,1)} %get-tuple-element.61.refs_3_, ...), custom_call_target="tpu_custom_call" | custom-call | flops 7864320000 | bytes 115343360 | tf_op jit(solution)/shard_map/adamw/pallas_call | solution.py:508
  627.0 40.0 %adamw_turned.2 = (bf16[2,5120,1024]{2,1,0:T(8,128)(2,1)}, f32[2,5120,1024]{2,1,0:T(8,128)}, f32[2,5120,1024]{2,1,0:T(8,128)}) custom-call(bf16[2,5120,1024]{2,1,0:T(8,128)(2,1)} %refs_0_.9, f32[2,5120,1024]{2,1,0:T(8,128)} %refs_1_.9, f32[2,5120,1024]{2,1,0:T(8,128)} %refs_2_.9, bf16[3,5,1024,512]{3,2,1,0:T(8,128)(2,1)} %get-tuple-element.61.refs_3_, ...), custom_call_target="tpu_custom_call" | custom-call | flops 7864320000 | bytes 115343360 | tf_op jit(solution)/shard_map/adamw_turned/pallas_call | solution.py:508
  667.0 12.4 %all-gather.7.cloned.1.call-done = bf16[64,32,5120]{2,1,0:T(8,128)(2,1)} async-done(((bf16[2,32,5120]{2,1,0:T(8,128)(2,1)}), bf16[64,32,5120]{2,1,0:T(8,128)(2,1)}) %all-gather.7.cloned.1.call-update) | async-done | bytes 20971536 | tf_op jit(solution)/shard_map/all_gather | solution.py:531
  679.4 38.1 %adamw.6 = (bf16[2,1024,5120]{2,1,0:T(8,128)(2,1)}, f32[2,1024,5120]{2,1,0:T(8,128)}, f32[2,1024,5120]{2,1,0:T(8,128)}) custom-call(bf16[2,1024,5120]{2,1,0:T(8,128)(2,1)} %refs_0_.10, f32[2,1024,5120]{2,1,0:T(8,128)} %refs_1_.10, f32[2,1024,5120]{2,1,0:T(8,128)} %refs_2_.10, ...), custom_call_target="tpu_custom_call", output_to_operand_aliasing={{0}: (4, {}), {1}: (5, {}), {2}: (6, {})} | custom-call | flops 7864320000 | bytes 115343360 | tf_op jit(solution)/shard_map/adamw/pallas_call | solution.py:508
  717.5 39.6 %adamw_turned.3 = (bf16[2,5120,1024]{2,1,0:T(8,128)(2,1)}, f32[2,5120,1024]{2,1,0:T(8,128)}, f32[2,5120,1024]{2,1,0:T(8,128)}) custom-call(bf16[2,5120,1024]{2,1,0:T(8,128)(2,1)} %refs_0_.9, f32[2,5120,1024]{2,1,0:T(8,128)} %refs_1_.9, f32[2,5120,1024]{2,1,0:T(8,128)} %refs_2_.9, ...), custom_call_target="tpu_custom_call", output_to_operand_aliasing={{0}: (4, {}), {1}: (5, {}), {2}: (6, {})} | custom-call | flops 7864320000 | bytes 115343360 | tf_op jit(solution)/shard_map/adamw_turned/pallas_call | solution.py:508
  757.0 9.7 %all-gather.5.cloned.1.call-done = bf16[32,32,5120]{2,1,0:T(8,128)(2,1)} async-done(((bf16[1,32,5120]{2,1,0:T(8,128)(2,1)}), bf16[32,32,5120]{2,1,0:T(8,128)(2,1)}) %all-gather.5.cloned.1.call-update) | async-done | bytes 10485776 | tf_op jit(solution)/shard_map/all_gather | solution.py:532
  766.7 38.0 %adamw.7 = (bf16[2,1024,5120]{2,1,0:T(8,128)(2,1)}, f32[2,1024,5120]{2,1,0:T(8,128)}, f32[2,1024,5120]{2,1,0:T(8,128)}) custom-call(bf16[2,1024,5120]{2,1,0:T(8,128)(2,1)} %refs_0_.11, f32[2,1024,5120]{2,1,0:T(8,128)} %refs_1_.11, f32[2,1024,5120]{2,1,0:T(8,128)} %refs_2_.11, ...), custom_call_target="tpu_custom_call", output_to_operand_aliasing={{0}: (4, {}), {1}: (5, {}), {2}: (6, {})} | custom-call | flops 7864320000 | bytes 115343360 | tf_op jit(solution)/shard_map/adamw/pallas_call | solution.py:508
Async XLA Ops:
  7.2 672.2 %all-gather.7.cloned.1.call-start = ((), (), s32[]{:S(2)}) async-start(), calls=%async_computation.1 | async-start | bytes 21626880 | tf_op jit(solution)/shard_map/all_gather | solution.py:531
  547.2 219.5 %all-gather.5.cloned.1.call-start = ((), (), s32[]{:S(2)}) async-start(), calls=%async_computation | async-start | bytes 10813440 | tf_op jit(solution)/shard_map/all_gather | solution.py:532
Sparse Core Ops, SparseCore 0:
  547.4 131.9 all-gather.6
  682.2 84.4 all-gather.4

commit v3 on v2

--- a/solution.py
+++ b/solution.py
@@ -23,6 +23,7 @@
 CHUNK = 512
 EARLY = 5
 WAIT = 2
+BEGIN = (0, 1, 0)
 
 
 def position(order, device):
@@ -203,8 +204,8 @@
 
 
 class Gather:
-    def __init__(self, n, first, load, begin, rows):
-        self.n, self.first, self.load, self.begin, self.rows = n, first, load, begin, rows
+    def __init__(self, n, first, load, begin, stride, rows):
+        self.n, self.first, self.load, self.begin, self.stride, self.rows = n, first, load, begin, stride, rows
 
     def scratch(self):
         return [
@@ -237,17 +238,21 @@
             device_id_type=MESH,
         )
 
-    def advance(self):
-        t = self.ex.j - self.load
-
-        @pl.when((t >= 0) & (t < self.n))
+    def chunk_at(self, step):
+        t = lax.div(step, self.stride)
+        return t, (step >= 0) & (t < self.n) & (lax.rem(step, self.stride) == 0)
+
+    def advance(self, step):
+        t, there = self.chunk_at(step - self.load)
+
+        @pl.when(there)
         def _():
             self.block[t] = self.part_ref[...]
 
         for k in reversed(range(STAGES + 1)):
-            t = self.ex.j - self.begin - k
-
-            @pl.when((t >= 0) & (t < self.n))
+            t, there = self.chunk_at(step - self.begin - k)
+
+            @pl.when(there)
             def _(k=k, t=t):
                 if k > 0:
                     copy = self.copy(k - 1, t)
@@ -302,7 +307,7 @@
     start_exchanges(exchanges, gathers, j, outs, [part_ref.at[i] for i in range(3)], all_ref, refs)
     more = j < down.n_c
     t = dy_ref.shape[0] // parts
-    gathers[0].advance()
+    gathers[0].advance(j)
     down.advance()
 
     @pl.when(more)
@@ -312,14 +317,14 @@
             by_mid = dot_nt(dy_ref[rows], wd_ref[0])
             mid_ref[rows], by_gate_ref[rows], by_up_ref[rows] = through(gate_ref[rows], up_ref[rows], by_mid)
 
-    gathers[1].advance()
+    gathers[1].advance(j)
     gate.advance()
 
     @pl.when(more)
     def _():
         down.put(dyt_ref.at[0], mid_ref[...])
 
-    gathers[2].advance()
+    gathers[2].advance(j)
     up.advance()
 
     @pl.when(more)
@@ -363,7 +368,7 @@
 
     for ex, g in zip(exchanges, gathers, strict=True):
         ex.advance()
-        g.advance()
+        g.advance(step)
 
     @pl.when(j < n_c)
     def _():
@@ -421,8 +426,11 @@
     ff = w_down.shape[1]
     n_c, rows = ff // CHUNK, d // GROUP
     exchanges = [Exchange(n_c, orders, rows) for orders in ORDERS]
-    chunks, first, load, begin = (EARLY, 0, STAGES, STAGES + WAIT) if kept is None else (n_c - EARLY, EARLY, 0, 0)
-    gathers = [Gather(chunks, first, load, begin, rows) for _ in ORDERS]
+    if kept is None:
+        gathers = [Gather(EARLY, 0, STAGES, STAGES + WAIT, 1, rows) for _ in ORDERS]
+    else:
+        gathers = [Gather(n_c - EARLY, EARLY, begin, begin, 2, rows) for begin in BEGIN]
+    chunks = gathers[0].n
     clip = lambda j: jnp.minimum(j, n_c - 1)
     dyt_spec, dy_t = piece(*dy_t)
     at_spec, a_t = piece(*a_t)
@@ -438,7 +446,7 @@
     out_shape = [jax.ShapeDtypeStruct((n, rows, ff), BF16) for n in parts] + [jax.ShapeDtypeStruct((3, chunks, d, CHUNK), BF16)]
     scratch = [pltpu.VMEM((tokens, CHUNK), BF16)]
     if kept is not None:
-        specs.append(pl.BlockSpec((3, rows, CHUNK), lambda j: (0, 0, EARLY + jnp.minimum(j, chunks - 1))))
+        specs.append(pl.BlockSpec((3, rows, CHUNK), lambda j: (0, 0, EARLY + jnp.minimum(lax.div(j, 2), chunks - 1))))
         args.append(part)
         scratch += scratch * 2
         grid = n_c + STAGES

time: 818 us -> 813 us (level)
  no operation moved by 1% of the time
where the time goes in v3:
time: 813 us; the launch traced here: 807 us
  Pallas kernels  769 us (95%)
  waiting for transfers between devices  23.3 us (3%)
  between operations  14.5 us (2%)
    pallas_call x2, Pallas kernels, backward(): pl.pallas_call(functools.partial(first_kernel if kept is not None else la...  445 us
    pallas_call x6, Pallas kernels, update(): pl.pallas_call(functools.partial(adamw_kernel, None if len(g) == 2 else O...  235 us
    pallas_call x1, Pallas kernels, forward(): pl.pallas_call(functools.partial(forward_kernel, 2), grid=(ff // CHUNK,),...  57.4 us
    pallas_call x1, Pallas kernels, down(): pl.pallas_call(down_kernel, grid=(tokens // rows,), in_specs=[pl.BlockSpe...  31.8 us
  transfers between devices with their start and end apart: 2, of which 2 were waited for; matrix products, arithmetic and copies ran while one was open for 0% of the time, Pallas kernels for 24%

profile of v3, /device:TPU:0, one launch (start us, length us, event | category | flops | bytes accessed | tf_op | source)
XLA Modules:
  0.0 807.2 jit_solution(10311277307822586021)
XLA Ops:
  7.2 0.0 all-gather.7.cloned.1.call-start
  7.2 57.4 %forward.1 = (f32[2048,5120]{1,0:T(8,128)}, f32[2048,5120]{1,0:T(8,128)}, bf16[2048,5120]{1,0:T(8,128)(2,1)}, bf16[2,1024,2048]{2,1,0:T(8,128)(2,1)}) custom-call(bf16[2048,1024]{1,0:T(8,128)(2,1)} %bitcast.10, bf16[2048,1024]{1,0:T(8,128)(2,1)} %bitcast.12, bf16[2,1024,5120]{2,1,0:T(8,128)(2,1)} %refs_0_.10, bf16[2,1024,5120]{2,1,0:T(8,128)(2,1)} %refs_0_.11), custom_call_target="tpu_custom_call" | custom-call | flops 42949672960 | bytes 104857600 | tf_op jit(solution)/shard_map/forward/pallas_call | solution.py:100
  64.7 31.8 %down.1 = (bf16[2048,1024]{1,0:T(8,128)(2,1)}, bf16[2048,1024]{1,0:T(8,128)(2,1)}, bf16[1024,2048]{1,0:T(8,128)(2,1)}) custom-call(bf16[2048,5120]{1,0:T(8,128)(2,1)} %get-tuple-element.50.mid_ref, bf16[2,5120,1024]{2,1,0:T(8,128)(2,1)} %refs_0_.9, bf16[2048,1024]{1,0:T(8,128)(2,1)} %bitcast.11), custom_call_target="tpu_custom_call" | custom-call | flops 21474836480 | bytes 31457280 | tf_op jit(solution)/shard_map/down/pallas_call | solution.py:126
  96.5 248.9 %last.1 = (bf16[3,32,5120]{2,1,0:T(8,128)(2,1)}, bf16[3,5,1024,512]{3,2,1,0:T(8,128)(2,1)}, bf16[2048,1024]{1,0:T(8,128)(2,1)}, bf16[1024,2048]{1,0:T(8,128)(2,1)}, bf16[10,2048,1024]{2,1,0:T(8,128)(2,1)}) custom-call(bf16[2048,1024]{1,0:T(8,128)(2,1)} %bitcast.13, bf16[2,2,512,2048]{3,2,1,0:T(8,128)(2,1)} %bitcast.14, bf16[1,2,512,2048]{3,2,1,0:T(8,128)(2,1)} %bitcast.17, ...), custom_call_target="tpu_custom_call" | custom-call | flops 171798691840 | bytes 83886080 | tf_op jit(solution)/shard_map/last/pallas_call | solution.py:464
  345.4 196.6 %first.1 = (bf16[2,32,5120]{2,1,0:T(8,128)(2,1)}, bf16[1,32,5120]{2,1,0:T(8,128)(2,1)}, bf16[3,5,1024,512]{3,2,1,0:T(8,128)(2,1)}) custom-call(bf16[2048,1024]{1,0:T(8,128)(2,1)} %get-tuple-element.54.dy_ref, bf16[1,2,512,2048]{3,2,1,0:T(8,128)(2,1)} %bitcast.16, bf16[2,2,512,2048]{3,2,1,0:T(8,128)(2,1)} %bitcast.15, ...), custom_call_target="tpu_custom_call" | custom-call | flops 85899345920 | bytes 83886080 | tf_op jit(solution)/shard_map/first/pallas_call | solution.py:464
  541.9 0.0 all-gather.7.cloned.1.call-update
  542.0 0.0 all-gather.5.cloned.1.call-start
  542.0 0.7 all-gather.5.cloned.1.call-update
  542.7 39.6 %adamw.5 = (bf16[2,1024,5120]{2,1,0:T(8,128)(2,1)}, f32[2,1024,5120]{2,1,0:T(8,128)}, f32[2,1024,5120]{2,1,0:T(8,128)}) custom-call(bf16[2,1024,5120]{2,1,0:T(8,128)(2,1)} %refs_0_.11, f32[2,1024,5120]{2,1,0:T(8,128)} %refs_1_.11, f32[2,1024,5120]{2,1,0:T(8,128)} %refs_2_.11, bf16[3,5,1024,512]{3,2,1,0:T(8,128)(2,1)} %get-tuple-element.61.refs_3_, ...), custom_call_target="tpu_custom_call" | custom-call | flops 7864320000 | bytes 115343360 | tf_op jit(solution)/shard_map/adamw/pallas_call | solution.py:516
  582.3 39.3 %adamw.4 = (bf16[2,1024,5120]{2,1,0:T(8,128)(2,1)}, f32[2,1024,5120]{2,1,0:T(8,128)}, f32[2,1024,5120]{2,1,0:T(8,128)}) custom-call(bf16[2,1024,5120]{2,1,0:T(8,128)(2,1)} %refs_0_.10, f32[2,1024,5120]{2,1,0:T(8,128)} %refs_1_.10, f32[2,1024,5120]{2,1,0:T(8,128)} %refs_2_.10, bf16[3,5,1024,512]{3,2,1,0:T(8,128)(2,1)} %get-tuple-element.61.refs_3_, ...), custom_call_target="tpu_custom_call" | custom-call | flops 7864320000 | bytes 115343360 | tf_op jit(solution)/shard_map/adamw/pallas_call | solution.py:516
  621.7 40.0 %adamw_turned.2 = (bf16[2,5120,1024]{2,1,0:T(8,128)(2,1)}, f32[2,5120,1024]{2,1,0:T(8,128)}, f32[2,5120,1024]{2,1,0:T(8,128)}) custom-call(bf16[2,5120,1024]{2,1,0:T(8,128)(2,1)} %refs_0_.9, f32[2,5120,1024]{2,1,0:T(8,128)} %refs_1_.9, f32[2,5120,1024]{2,1,0:T(8,128)} %refs_2_.9, bf16[3,5,1024,512]{3,2,1,0:T(8,128)(2,1)} %get-tuple-element.61.refs_3_, ...), custom_call_target="tpu_custom_call" | custom-call | flops 7864320000 | bytes 115343360 | tf_op jit(solution)/shard_map/adamw_turned/pallas_call | solution.py:516
  661.7 12.9 %all-gather.7.cloned.1.call-done = bf16[64,32,5120]{2,1,0:T(8,128)(2,1)} async-done(((bf16[2,32,5120]{2,1,0:T(8,128)(2,1)}), bf16[64,32,5120]{2,1,0:T(8,128)(2,1)}) %all-gather.7.cloned.1.call-update) | async-done | bytes 20971536 | tf_op jit(solution)/shard_map/all_gather | solution.py:539
  674.6 38.1 %adamw.6 = (bf16[2,1024,5120]{2,1,0:T(8,128)(2,1)}, f32[2,1024,5120]{2,1,0:T(8,128)}, f32[2,1024,5120]{2,1,0:T(8,128)}) custom-call(bf16[2,1024,5120]{2,1,0:T(8,128)(2,1)} %refs_0_.10, f32[2,1024,5120]{2,1,0:T(8,128)} %refs_1_.10, f32[2,1024,5120]{2,1,0:T(8,128)} %refs_2_.10, ...), custom_call_target="tpu_custom_call", output_to_operand_aliasing={{0}: (4, {}), {1}: (5, {}), {2}: (6, {})} | custom-call | flops 7864320000 | bytes 115343360 | tf_op jit(solution)/shard_map/adamw/pallas_call | solution.py:516
  712.7 39.6 %adamw_turned.3 = (bf16[2,5120,1024]{2,1,0:T(8,128)(2,1)}, f32[2,5120,1024]{2,1,0:T(8,128)}, f32[2,5120,1024]{2,1,0:T(8,128)}) custom-call(bf16[2,5120,1024]{2,1,0:T(8,128)(2,1)} %refs_0_.9, f32[2,5120,1024]{2,1,0:T(8,128)} %refs_1_.9, f32[2,5120,1024]{2,1,0:T(8,128)} %refs_2_.9, ...), custom_call_target="tpu_custom_call", output_to_operand_aliasing={{0}: (4, {}), {1}: (5, {}), {2}: (6, {})} | custom-call | flops 7864320000 | bytes 115343360 | tf_op jit(solution)/shard_map/adamw_turned/pallas_call | solution.py:516
  752.3 9.7 %all-gather.5.cloned.1.call-done = bf16[32,32,5120]{2,1,0:T(8,128)(2,1)} async-done(((bf16[1,32,5120]{2,1,0:T(8,128)(2,1)}), bf16[32,32,5120]{2,1,0:T(8,128)(2,1)}) %all-gather.5.cloned.1.call-update) | async-done | bytes 10485776 | tf_op jit(solution)/shard_map/all_gather | solution.py:540
  762.0 38.0 %adamw.7 = (bf16[2,1024,5120]{2,1,0:T(8,128)(2,1)}, f32[2,1024,5120]{2,1,0:T(8,128)}, f32[2,1024,5120]{2,1,0:T(8,128)}) custom-call(bf16[2,1024,5120]{2,1,0:T(8,128)(2,1)} %refs_0_.11, f32[2,1024,5120]{2,1,0:T(8,128)} %refs_1_.11, f32[2,1024,5120]{2,1,0:T(8,128)} %refs_2_.11, ...), custom_call_target="tpu_custom_call", output_to_operand_aliasing={{0}: (4, {}), {1}: (5, {}), {2}: (6, {})} | custom-call | flops 7864320000 | bytes 115343360 | tf_op jit(solution)/shard_map/adamw/pallas_call | solution.py:516
Async XLA Ops:
  7.2 667.4 %all-gather.7.cloned.1.call-start = ((), (), s32[]{:S(2)}) async-start(), calls=%async_computation.1 | async-start | bytes 21626880 | tf_op jit(solution)/shard_map/all_gather | solution.py:539
  542.0 220.0 %all-gather.5.cloned.1.call-start = ((), (), s32[]{:S(2)}) async-start(), calls=%async_computation | async-start | bytes 10813440 | tf_op jit(solution)/shard_map/all_gather | solution.py:540
Sparse Core Ops, SparseCore 0:
  542.1 132.4 all-gather.6
  677.5 84.4 all-gather.4
